TPU v7x, 8 devices: a whole 2x2x1 slice. The times are simulated.
8 devices in a mesh: model: 1 (over z), replica: 2 (over y), fsdp: 4 (over x, core).
Axes of the slice: x: 2, y: 2, z: 1, core: 2. Of those that a mesh axis runs over, the one named last changes fastest.
Arguments:
- x_in: bfloat16 [2, 16384, 1024], P(None, ('model', 'replica', 'fsdp'))
- dy_out: bfloat16 [2, 16384, 1024], P(None, ('model', 'replica', 'fsdp'))
- lengths: int32 [2, 8], P(None, ('model', 'replica', 'fsdp'))
- w_up: bfloat16 [4, 1024, 4096], P(None, ('model', 'fsdp'))
- w_down: bfloat16 [4, 4096, 1024], P(None, ('model', 'fsdp'))
Outputs:
- output 1: float32 [4, 1024, 4096], P(None, ('model', 'fsdp'))
- output 2: float32 [4, 4096, 1024], P(None, ('model', 'fsdp'))
All inputs are finite; a program needn't handle non-finite values.
Results may differ from a plain program's by a relative error of at most 0.00910575.
Values are sent between devices in bfloat16 or wider.
A program may use at most 1 GiB of HBM per device.

v0:
```python
import jax
import jax.numpy as jnp
from jax import lax
from jax.experimental import pallas as pl
from jax.experimental.pallas import tpu as pltpu
from jax.sharding import PartitionSpec as P


BF = jnp.bfloat16
F32 = jnp.float32
BLK = 32
TB = 512
NBUF = 3
K0 = 0.7978845608028654
K1 = 0.044715
TYP = 3584
SWAP_CORE = [(0, 1), (1, 0), (2, 3), (3, 2)]
SWAP_X = [(0, 2), (2, 0), (1, 3), (3, 1)]
WHOLE = (0, 3, 5, 6, 7)
CLASS_STEP = (1, 4, 5)
ANY = pl.BlockSpec(memory_space=pl.ANY)
NT = (((1,), (1,)), ((), ()))
TN = (((0,), (0,)), ((), ()))


def gelu_of(h):
    return h * (0.5 + 0.5 * jnp.tanh(h * (K0 + (K0 * K1) * (h * h))))


def gelu_grad_of(h):
    hh = h * h
    s = 0.5 + 0.5 * jnp.tanh(h * (K0 + (K0 * K1) * hh))
    return s + ((s * (1.0 - s)) * h) * ((2.0 * K0) + (6.0 * K0 * K1) * hh)


def load_weight(meta, layer, parts, w, sem, first=0):
    own, par, *far = parts
    x, c, y = meta[0], meta[1], meta[2]
    unit = own.shape[1]
    half = unit // 2
    o = 1 - x
    mine, other = (2 * o + c) * unit, (2 * o + 1 - c) * unit
    rows = [(own.at[layer], (2 * x + c) * unit, unit), (par.at[layer], (2 * x + 1 - c) * unit, unit)]
    if len(far) == 2:
        rows += [(far[0], mine, unit), (far[1], other, unit)]
    else:
        low, high = y * half, (1 - y) * half
        rows += [(far[0], mine + low, half), (far[1], mine + high, half)]
        rows += [(far[2], other + low, half), (far[3], other + high, half)]
    size = w.shape[0]

    def each(act):
        for k, (src, row, n) in enumerate(rows):
            if size == 4 * unit:
                at = pl.multiple_of(row, half)
                act(pltpu.make_async_copy(src, w.at[pl.ds(at, n)], sem.at[k]))
            else:
                @pl.when(row // size == first)
                def _(src=src, row=row, n=n, k=k):
                    at = pl.multiple_of(row - first * size, half)
                    act(pltpu.make_async_copy(src, w.at[pl.ds(at, n)], sem.at[k]))

    each(lambda cp: cp.start())
    each(lambda cp: cp.wait())


def tile(rows, cols, col=None):
    pick = col or (lambda m: 0)
    return pl.BlockSpec((rows, cols), lambda t, m: (jnp.minimum(t, m[5] - 1), pick(m)))


def call(body, grid, in_specs, out_specs, out_shape, args, deps, scratch, flops, nbytes, aliases=None):
    n_in, n_dep, n_out = len(args), len(deps), len(out_shape)

    def kern(meta, *refs):
        rest = refs[n_in + n_dep:]
        body(meta, refs[:n_in], rest[:n_out], rest[n_out + 1:])

    def run(meta):
        return pl.pallas_call(
            kern,
            grid_spec=pltpu.PrefetchScalarGridSpec(
                num_scalar_prefetch=1,
                grid=grid,
                in_specs=list(in_specs) + [ANY] * n_dep,
                out_specs=list(out_specs) + [ANY],
                scratch_shapes=scratch,
            ),
            out_shape=list(out_shape) + [jax.ShapeDtypeStruct((8, 128), F32)],
            input_output_aliases=aliases or {},
            cost_estimate=pl.CostEstimate(flops=flops, bytes_accessed=nbytes, transcendentals=0),
            compiler_params=pltpu.CompilerParams(
                dimension_semantics=("arbitrary",) * len(grid), vmem_limit_bytes=67043328
            ),
        )(meta, *args, *deps)

    return run


def live_tiles(meta, t, compute):
    @pl.when(t < meta[6])
    def _():
        compute(slice(0, TB))

    @pl.when((t >= meta[6]) & (t < meta[5]))
    def _():
        compute(slice(0, TB // 2))


def gradient_out(t, last_live, last, acc, dsts, sem):
    n = acc.shape[1] // len(dsts)
    copies = [
        pltpu.make_async_copy(acc.at[:, pl.ds(k * n, n)], dst, sem.at[k]) for k, dst in enumerate(dsts)
    ]

    @pl.when(t == last_live)
    def _():
        for cp in copies:
            cp.start()

    @pl.when(t == last)
    def _():
        for cp in copies:
            cp.wait()


def blocks_of(cls, n_blk):
    low = n_blk // 2
    first = [b for b in range(low) if b % 2 == cls]
    return first + [b for b in range(low, n_blk) if (b - low) % 4 == cls]


def count_of(length, cls, tok):
    low = jnp.minimum(length, tok // 2)
    high = length - low

    def share(n, ways):
        return (n // (ways * BLK)) * BLK + jnp.clip(n % (ways * BLK) - cls * BLK, 0, BLK)

    return (share(low, 2) if cls < 2 else 0) + share(high, 4)


def split(v, deps=()):
    n_micro, n_blk, blk, d = v.shape
    lists = [blocks_of(cls, n_blk) for cls in (1, 2, 3)]

    def body(meta, ins, outs, scr):
        bufs, isem, osem = scr[:3], scr[3], scr[4]
        takes = [
            [
                pltpu.make_async_copy(ins[0].at[k, b], buf.at[k, pl.ds(n * blk, blk)], isem.at[c])
                for k in range(n_micro) for n, b in enumerate(lists[c])
            ]
            for c, buf in enumerate(bufs)
        ]
        gives = [pltpu.make_async_copy(buf, o, osem.at[c]) for c, (buf, o) in enumerate(zip(bufs, outs))]
        order = (1, 2, 0)
        for c in order:
            for cp in takes[c]:
                cp.start()
        for c in order:
            for cp in takes[c]:
                cp.wait()
            gives[c].start()
        for cp in gives:
            cp.wait()

    shapes = [(n_micro, len(x) * blk, d) for x in lists]
    return call(
        body, (1,), [ANY], [ANY] * 3, [jax.ShapeDtypeStruct(s, BF) for s in shapes], (v,), deps,
        [pltpu.VMEM(s, BF) for s in shapes] + [pltpu.SemaphoreType.DMA((3,))] * 2,
        TYP * d * 1000, n_micro * n_blk * blk * d * 3,
    )(jnp.zeros((1,), jnp.int32))


def pack(meta, v, gots, masked, deps=()):
    n_micro, n_blk, blk, d = v.shape
    mine = blocks_of(0, n_blk)
    total = n_micro * n_blk * blk
    seqs = [(None, k) for k in range(n_micro)] + [(c, k) for c in range(len(gots)) for k in range(n_micro)]
    longest = len(mine) * blk

    def body(meta, ins, outs, scr):
        v_hbm, *got = ins
        (o_hbm,) = outs
        buf, zero, isem, osem = scr
        takes = []
        for s, (c, k) in enumerate(seqs):
            if c is None:
                takes.append([
                    pltpu.make_async_copy(v_hbm.at[k, b], buf.at[s, pl.ds(n * blk, blk)], isem.at[s])
                    for n, b in enumerate(mine)
                ])
            else:
                n = gots[c].shape[1]
                takes.append([pltpu.make_async_copy(got[c].at[k], buf.at[s, pl.ds(0, n)], isem.at[s])])
        for copies in takes:
            for cp in copies:
                cp.start()
        zero[...] = jnp.zeros_like(zero)

        def pieces(src, off, n, largest):
            at, out = jnp.int32(0), []
            size = largest
            while size >= 16:
                on = (n // size) % 2 == 1
                here = pl.ds(pl.multiple_of(at, 16), size) if src is not zero else pl.ds(0, size)
                there = pl.ds(pl.multiple_of(off + at, 16), size)
                out.append((on, pltpu.make_async_copy(src.at[here], o_hbm.at[there], osem)))
                at = at + jnp.where(on, size, 0)
                size //= 2
            return out

        gives, off = [], jnp.int32(0)
        for s in range(len(seqs)):
            n = meta[8 + s]
            for cp in takes[s]:
                cp.wait()
            if masked:
                base = n // 16 * 16

                @pl.when(n > base)
                def _(s=s, n=n, base=base):
                    row = pl.ds(pl.multiple_of(base, 16), 16)
                    at = lax.broadcasted_iota(jnp.int32, (16, d), 0) + base
                    buf[s, row, :] = jnp.where(at < n, buf[s, row, :].astype(F32), 0.0).astype(BF)

            n = (n + 15) // 16 * 16
            for on, cp in pieces(buf.at[s], off, n, 512):
                gives.append((on, cp))
                pl.when(on)(cp.start)
            off = off + n
        for on, cp in pieces(zero, off, meta[5] * TB - off, 256):
            gives.append((on, cp))
            pl.when(on)(cp.start)
        for on, cp in gives:
            pl.when(on)(cp.wait)

    return call(
        body, (1,), [ANY] * (1 + len(gots)), [ANY], [jax.ShapeDtypeStruct((total, d), BF)], (v,) + tuple(gots), deps,
        [pltpu.VMEM((len(seqs), longest, d), BF), pltpu.VMEM((TB // 2, d), BF), pltpu.SemaphoreType.DMA((len(seqs),)),
         pltpu.SemaphoreType.DMA(())],
        TYP * d * 2000, total * d * 4,
    )(meta)


def fwd_up(meta, xc, wts, layer, dy=None, n_p=1, deps=()):
    d, f = xc.shape[1], wts[0].shape[2]
    ch = 512
    steps = xc.shape[0] // TB
    fused = dy is not None
    n_w = len(wts)

    def body(meta, ins, outs, scr):
        x_ref = ins[0]
        parts = ins[1:1 + n_w]
        h_ref, a_ref = outs[:2]
        w, sem = scr[:2]
        t = pl.program_id(0)

        def activate(j, rs):
            sl = slice(j * ch, (j + 1) * ch)
            a_ref[rs, sl] = gelu_of(h_ref[rs, sl].astype(F32)).astype(BF)

        def share(i, rs):
            acc = scr[2]
            g = ins[1 + n_w][rs, :]
            col = pl.multiple_of((2 * i + 1 - meta[1]) * (f // 4), f // 4)
            part = lax.dot_general(a_ref[rs, pl.ds(col, f // 4)], g, TN, preferred_element_type=F32)
            acc[i] = part + jnp.where(t == 0, 0.0, acc[i])

        @pl.when(t == 0)
        def _():
            load_weight(meta, layer, parts, w, sem)

        def compute(rs):
            x = x_ref[rs, :]
            n = f // ch
            for j in range(n):
                sl = slice(j * ch, (j + 1) * ch)
                h_ref[rs, sl] = jnp.dot(x, w[:, sl], preferred_element_type=F32).astype(BF)
                if j:
                    activate(j - 1, rs)
                if fused and j == n // 2 + 1:
                    share(0, rs)
            activate(n - 1, rs)
            if fused:
                share(1, rs)

        live_tiles(meta, t, compute)

        if fused:
            gradient_out(t, meta[5] - 1, steps - 1, scr[2], outs[2:], scr[3])

    out = jax.ShapeDtypeStruct((xc.shape[0], f), BF)
    more_in, more_spec, more_out, more_ospec, more_scr = (), [], [], [], []
    if fused:
        shape = (2, f // 4, d)
        more_in, more_spec = (dy,), [tile(TB, d)]
        more_out = [jax.ShapeDtypeStruct((2, f // 4 // n_p, d), F32)] * n_p
        more_ospec = [ANY] * n_p
        more_scr = [pltpu.VMEM(shape, F32), pltpu.SemaphoreType.DMA((n_p,))]
    return call(
        body, (steps,), [tile(TB, d)] + [ANY] * n_w + more_spec, [tile(TB, f)] * 2 + more_ospec,
        [out, out] + more_out, (xc,) + wts + more_in, deps,
        [pltpu.VMEM((d, f), BF), pltpu.SemaphoreType.DMA((6,))] + more_scr,
        (3 if fused else 2) * TYP * d * f, TYP * (d + 2 * f) * 2,
    )(meta)


def fwd_down(meta, xc, a, wts, layer, deps=()):
    d, f = xc.shape[1], a.shape[1]
    ch = 512

    def body(meta, ins, outs, scr):
        x_ref, a_ref, *parts = ins
        (o_ref,) = outs
        w, sem = scr
        t = pl.program_id(0)

        @pl.when(t == 0)
        def _():
            load_weight(meta, layer, parts, w, sem)

        def compute(rs):
            for j in range(d // ch):
                sl = slice(j * ch, (j + 1) * ch)
                y = jnp.dot(a_ref[rs, :], w[:, sl], preferred_element_type=F32)
                o_ref[rs, sl] = (x_ref[rs, sl].astype(F32) + y).astype(BF)

        live_tiles(meta, t, compute)

    return call(
        body, (xc.shape[0] // TB,), [tile(TB, d), tile(TB, f)] + [ANY] * len(wts), [tile(TB, d)],
        [jax.ShapeDtypeStruct(xc.shape, BF)], (xc, a) + wts, deps,
        [pltpu.VMEM((f, d), BF), pltpu.SemaphoreType.DMA((6,))],
        2 * TYP * d * f, TYP * (2 * d + f) * 2,
    )(meta)


def fwd_layer(meta, xc, ups, downs, layer, deps=()):
    d, f = xc.shape[1], ups[0].shape[2]
    ch = 512
    n_up, n_w = len(ups), len(ups) + len(downs)

    def body(meta, ins, outs, scr):
        x_ref, *parts = ins
        h_ref, a_ref, o_ref = outs
        wu, wd, usem, dsem = scr
        t = pl.program_id(0)

        @pl.when(t == 0)
        def _():
            load_weight(meta, layer, parts[:n_up], wu, usem)
            load_weight(meta, layer, parts[n_up:], wd, dsem)

        def activate(j, rs):
            sl = slice(j * ch, (j + 1) * ch)
            a_ref[rs, sl] = gelu_of(h_ref[rs, sl].astype(F32)).astype(BF)

        def compute(rs):
            x = x_ref[rs, :]
            n = f // ch
            for j in range(n):
                sl = slice(j * ch, (j + 1) * ch)
                h_ref[rs, sl] = jnp.dot(x, wu[:, sl], preferred_element_type=F32).astype(BF)
                if j:
                    activate(j - 1, rs)
            activate(n - 1, rs)
            for j in range(d // ch):
                sl = slice(j * ch, (j + 1) * ch)
                y = jnp.dot(a_ref[rs, :], wd[:, sl], preferred_element_type=F32)
                o_ref[rs, sl] = (x_ref[rs, sl].astype(F32) + y).astype(BF)

        live_tiles(meta, t, compute)

    out = jax.ShapeDtypeStruct((xc.shape[0], f), BF)
    return call(
        body, (xc.shape[0] // TB,), [tile(TB, d)] + [ANY] * n_w, [tile(TB, f), tile(TB, f), tile(TB, d)],
        [out, out, jax.ShapeDtypeStruct(xc.shape, BF)], (xc,) + ups + downs, deps,
        [pltpu.VMEM((d, f), BF), pltpu.VMEM((f, d), BF),
         pltpu.SemaphoreType.DMA((6,)), pltpu.SemaphoreType.DMA((6,))],
        4 * TYP * d * f, TYP * (2 * d + 2 * f) * 2,
    )(meta)


def bwd_hidden(meta, dx, h, xl, wts, layer, part=0, n_parts=1, deps=()):
    d, f = dx.shape[1], h.shape[1] // n_parts
    ch = 512
    steps = dx.shape[0] // TB

    def body(meta, ins, outs, scr):
        dx_ref, h_ref, x0, x1, *parts = ins
        o_ref, share = outs
        w, acc, sem, osem = scr
        t = pl.program_id(0)

        @pl.when(t == 0)
        def _():
            load_weight(meta, layer, parts, w, sem, part)

        def add(j, rs):
            sl = slice(j * ch, (j + 1) * ch)
            for i, x_ref in enumerate((x0, x1)):
                part = lax.dot_general(x_ref[rs, :], o_ref[rs, sl], TN, preferred_element_type=F32)
                acc[i, :, sl] = part + jnp.where(t == 0, 0.0, acc[i, :, sl])

        def compute(rs):
            g = dx_ref[rs, :]
            n = f // ch
            for j in range(n):
                sl = slice(j * ch, (j + 1) * ch)
                da = lax.dot_general(g, w[sl, :], NT, preferred_element_type=F32)
                o_ref[rs, sl] = (da * gelu_grad_of(h_ref[rs, sl].astype(F32))).astype(BF)
                if j:
                    add(j - 1, rs)
            add(n - 1, rs)

        live_tiles(meta, t, compute)

        gradient_out(t, meta[5] - 1, steps - 1, acc, [share], osem)

    u = d // 4
    return call(
        body, (steps,),
        [tile(TB, d), tile(TB, f, lambda m: part), tile(TB, u, lambda m: 1 - m[1]), tile(TB, u, lambda m: 3 - m[1])]
        + [ANY] * len(wts),
        [tile(TB, f), ANY],
        [jax.ShapeDtypeStruct((h.shape[0], f), BF), jax.ShapeDtypeStruct((2, u, f), F32)], (dx, h, xl, xl) + wts, deps,
        [pltpu.VMEM((f, d), BF), pltpu.VMEM((2, u, f), F32), pltpu.SemaphoreType.DMA((6,)), pltpu.SemaphoreType.DMA((1,))],
        3 * TYP * d * f, TYP * (d + 2 * f) * 2,
    )(meta)


def bwd_input(meta, dx, dhs, a, wts, layer, deps=()):
    d, f = dx.shape[1], 2 * dhs[0].shape[1]
    ch = 256
    steps = dx.shape[0] // TB
    u = f // 4

    def body(meta, ins, outs, scr):
        dx_ref, dh0, dh1, a0, a1, *parts = ins
        o_ref, share = outs
        w, acc, sem, osem = scr
        t = pl.program_id(0)

        @pl.when(t == 0)
        def _():
            load_weight(meta, layer, parts, w, sem)

        def compute(rs):
            for j in range(d // ch):
                sl = slice(j * ch, (j + 1) * ch)
                y = lax.dot_general(dh0[rs, :], w[sl, :f // 2], NT, preferred_element_type=F32)
                y = y + lax.dot_general(dh1[rs, :], w[sl, f // 2:], NT, preferred_element_type=F32)
                o_ref[rs, sl] = (dx_ref[rs, sl].astype(F32) + y).astype(BF)
            for i, a_ref in enumerate((a0, a1)):
                for r in range(0, u, 256):
                    part = lax.dot_general(a_ref[rs, r:r + 256], o_ref[rs, :], TN, preferred_element_type=F32)
                    acc[i, r:r + 256, :] = part + jnp.where(t == 0, 0.0, acc[i, r:r + 256, :])

        live_tiles(meta, t, compute)

        gradient_out(t, meta[5] - 1, steps - 1, acc, [share], osem)

    return call(
        body, (steps,),
        [tile(TB, d), tile(TB, f // 2), tile(TB, f // 2), tile(TB, u, lambda m: 1 - m[1]), tile(TB, u, lambda m: 3 - m[1])]
        + [ANY] * len(wts),
        [tile(TB, d), ANY],
        [jax.ShapeDtypeStruct(dx.shape, BF), jax.ShapeDtypeStruct((2, u, d), F32)], (dx, *dhs, a, a) + wts, deps,
        [pltpu.VMEM((d, f), BF), pltpu.VMEM((2, u, d), F32), pltpu.SemaphoreType.DMA((6,)), pltpu.SemaphoreType.DMA((1,))],
        3 * TYP * d * f, TYP * (2 * d + f) * 2,
    )(meta)


def grad(meta, kind, which, v, g, p, n_p, share, moved, deps=()):
    d = g.shape[1] if kind == "d" else v.shape[1]
    f = v.shape[1] if kind == "d" else g.shape[1]
    rows, cols = (f // 4 // n_p, d) if kind == "d" else (d // 4, f // n_p)
    adds = (share,) if moved is None else (share, moved)
    n_add = len(adds)

    def body(meta, ins, outs, scr):
        v_hbm, g_hbm = ins[:2]
        vbuf, gbuf, acc, ebuf, vsem, gsem, esem, osem = scr
        x, c, nb = meta[0], meta[1], meta[5]
        xb = x if which == "K" else 1 - x
        shard = 2 * xb + c

        def copies(t, slot):
            row = pl.ds(pl.multiple_of(t * TB, TB), TB)
            col = (shard * n_p + p) * rows if kind == "d" else shard * rows
            v_src = v_hbm.at[row, pl.ds(pl.multiple_of(col, rows), rows)]
            g_src = g_hbm.at[row] if kind == "d" else g_hbm.at[row, pl.ds(p * cols, cols)]
            return [
                pltpu.make_async_copy(v_src, vbuf.at[slot], vsem.at[slot]),
                pltpu.make_async_copy(g_src, gbuf.at[slot], gsem.at[slot]),
            ]

        def fetch(t, slot):
            for cp in copies(t, slot):
                cp.start()

        for k in range(NBUF - 1):
            @pl.when(k < nb)
            def _(k=k):
                fetch(k, k)

        if share.shape[1:] == (rows, cols):
            src = ins[2].at[xb]
        elif kind == "d":
            src = ins[2].at[xb, pl.ds(p * rows, rows)]
        else:
            src = ins[2].at[xb, :, pl.ds(p * cols, cols)]
        adding = [pltpu.make_async_copy(src, ebuf.at[0], esem.at[0])]
        if moved is not None:
            adding.append(pltpu.make_async_copy(ins[3], ebuf.at[1], esem.at[1]))
        if kind == "d":
            tiles = [(pl.ds(r, 256), pl.ds(0, cols)) for r in range(0, rows, 256)]
        else:
            tiles = [(pl.ds(0, rows), pl.ds(k, 1024)) for k in range(0, cols, 1024)]

        def send(rs, cs):
            return pltpu.make_async_copy(acc.at[rs, cs], outs[0].at[rs, cs], osem)

        def step(t, final, tokens=TB):
            slot = lax.rem(t, NBUF)
            nxt = t + NBUF - 1

            @pl.when(nxt < nb)
            def _():
                fetch(nxt, lax.rem(nxt, NBUF))

            for cp in copies(t, slot):
                cp.wait()

            @pl.when(t == 0)
            def _():
                for cp in adding:
                    cp.start()

            if final:
                for cp in adding:
                    cp.wait()
            for n, (rs, cs) in enumerate(tiles):
                part = lax.dot_general(
                    vbuf[slot, :tokens, rs], gbuf[slot, :tokens, cs], TN, preferred_element_type=F32
                )
                part = part + jnp.where(t == 0, 0.0, acc[rs, cs])
                if final:
                    for k in range(n_add):
                        part = part + ebuf[k, rs, cs]
                acc[rs, cs] = part
                if final and n:
                    send(*tiles[n - 1]).start()
            if final:
                send(*tiles[-1]).start()

        def loop(t, carry):
            step(t, False)
            return carry

        lax.fori_loop(0, nb - 1, loop, 0)
        whole = meta[6] == nb
        for tokens, here in ((TB, whole), (TB // 2, jnp.logical_not(whole))):
            @pl.when(here)
            def _(tokens=tokens):
                step(nb - 1, True, tokens)

        for part in tiles:
            send(*part).wait()

    scratch = [
        pltpu.VMEM((NBUF, TB, rows), BF),
        pltpu.VMEM((NBUF, TB, cols), BF),
        pltpu.VMEM((rows, cols), F32),
        pltpu.VMEM((n_add, rows, cols), F32),
        pltpu.SemaphoreType.DMA((NBUF,)),
        pltpu.SemaphoreType.DMA((NBUF,)),
        pltpu.SemaphoreType.DMA((2,)),
        pltpu.SemaphoreType.DMA(()),
    ]
    return call(
        body, (1,), [ANY] * (2 + n_add), [ANY], [jax.ShapeDtypeStruct((rows, cols), F32)], (v, g) + adds, deps, scratch,
        TYP * d * f // 2 // n_p, TYP * (d + f) // n_p * 2,
    )(meta)


def finish(meta, buf, mine, theirs, shape, layer, row, col, deps=()):
    rows, cols = mine.shape
    br, bc = min(rows, 256), min(cols, 1024)

    def body(meta, ins, outs, scr):
        outs[0][0] = ins[0][...] + ins[1][...]

    args = (mine, theirs) if buf is None else (mine, theirs, buf)
    part = pl.BlockSpec((br, bc), lambda i, j, m: (i, j))
    return call(
        body, (rows // br, cols // bc), [part, part] + [ANY] * (len(args) - 2),
        [pl.BlockSpec((1, br, bc), lambda i, j, m: (layer, row // br + i, col // bc + j))],
        [jax.ShapeDtypeStruct(shape, F32)], args, deps, [], 0, rows * cols * 12,
        None if buf is None else {3: 0},
    )(meta)


PIECES = {("d", 3): 2, ("d", 0): 2, ("u", 0): 4, ("u", 3): 2, ("u", 2): 2, ("u", 1): 2}
ORDER = [
    ("S", "d", 3, 0), ("B1", 3, 1), ("S", "d", 3, 1), ("S", "u", 3, 1), ("B1", 3, 0), ("K", "d", 3, 1), ("dx", 3),
    ("S", "u", 3, 0), ("K", "d", 3, 0), ("K", "u", 3, 1), ("S", "d", 2, 0), ("B1", 2, 1), ("K", "u", 3, 0),
    ("B1", 2, 0), ("S", "u", 2, 1), ("S", "u", 2, 0), ("K", "d", 2, 0), ("dx", 2), ("K", "u", 2, 1),
    ("S", "d", 1, 0), ("B1", 1, 0), ("K", "u", 2, 0), ("B1", 1, 1), ("K", "d", 1, 0), ("S", "u", 1, 1),
    ("S", "u", 1, 0), ("dx", 1), ("K", "u", 1, 1), ("S", "d", 0, 1), ("S", "d", 0, 0), ("K", "u", 1, 0),
    ("B1", 0, 1), ("K", "d", 0, 1), ("B1", 0, 0), ("K", "d", 0, 0), ("S", "u", 0, 0), ("S", "u", 0, 3),
    ("S", "u", 0, 1), ("PUT", "u", 3, 1), ("PUT", "d", 3, 1), ("K", "u", 0, 0), ("PUT", "u", 2, 1),
    ("PUT", "d", 0, 1), ("PUT", "d", 2, 0), ("K", "u", 0, 3), ("S", "u", 0, 2), ("PUT", "u", 0, 0),
    ("PUT", "u", 1, 1), ("K", "u", 0, 1), ("PUT", "d", 0, 0), ("PUT", "d", 3, 0), ("PUT", "u", 1, 0),
    ("K", "u", 0, 2), ("PUT", "u", 0, 3), ("PUT", "u", 3, 0), ("PUT", "u", 2, 0), ("PUT", "u", 0, 1),
    ("PUT", "d", 1, 0), ("PUT", "u", 0, 2),
]


def pieces_of(kind, layer):
    return PIECES.get((kind, layer), 1)


def solution(mesh):
    tok_spec = P(None, ("model", "replica", "fsdp"), None)
    len_spec = P(None, ("model", "replica", "fsdp"))
    w_spec = P(None, ("model", "fsdp"), None)

    def device_grads(x_in, dy_out, lengths, w_up, w_down):
        n_micro, tok, d = x_in.shape
        n_layers, unit_d, f = w_up.shape
        unit_f = w_down.shape[1]
        fi = lax.axis_index("fsdp")
        yi = lax.axis_index("replica")

        def swap(v):
            return lax.ppermute(v, "fsdp", SWAP_CORE)

        def swap_y(v):
            return lax.ppermute(v, "replica", [(0, 1), (1, 0)])

        mats = [(w, l) for l in range(n_layers) for w in (w_up, w_down)]

        def half(w, l):
            n = w.shape[1] // 2
            return lax.dynamic_slice(w, (l, yi * n, 0), (1, n, w.shape[2]))[0]

        held = {id(w): lax.optimization_barrier(w) for w in (w_up, w_down)}
        far_x = []
        for i, (w, l) in enumerate(mats):
            src = w[l] if i == 0 else held[id(w)][l] if i in WHOLE else half(held[id(w)], l)
            far_x.append(lax.ppermute(src, "fsdp", SWAP_X))
        par = {}
        for w in (w_up, w_down):
            par[id(w)] = swap(w)
        parts = []
        for i, (w, l) in enumerate(mats):
            far = [far_x[i]]
            if i not in WHOLE:
                far.append(swap_y(far_x[i]))
            far.append(swap(far_x[i]))
            if i not in WHOLE:
                far.append(swap(far[1]))
            parts.append((w, par[id(w)], *far))
        ups, downs = parts[0::2], parts[1::2]

        def to_class(v, cls):
            step = CLASS_STEP[cls - 1]
            return lax.ppermute(v, ("replica", "fsdp"), [(i, i ^ step) for i in range(8)])

        lens = [lengths[:, 0]]
        for cls in (1, 2, 3):
            lens.append(to_class(lengths, cls)[:, 0])
        counts = [count_of(lens[cls], cls, tok)[k] for cls in range(4) for k in range(n_micro)]
        total = sum((n + 15) // 16 for n in counts)
        n_tok = total * 16
        nb = (n_tok + TB - 1) // TB
        n_full = (n_tok + TB // 2 - 1) // TB
        meta = jnp.stack([fi // 2, fi % 2, yi, n_tok, nb, nb, n_full, nb] + counts).astype(jnp.int32)

        def exchange(v, deps):
            v = v.reshape(n_micro, tok // BLK, BLK, d)
            *parts, done = split(v, deps=deps)
            gots = []
            for cls in (1, 2, 3):
                gots.append(to_class(parts[cls - 1], cls))
            return v, gots, done

        x_own, x_gots, tok_ = exchange(x_in, ())
        dy_own, dy_gots, tok_ = exchange(dy_out, (tok_,))
        xc, tok_ = pack(meta, x_own, x_gots, False, deps=(tok_,))
        dxs = {}

        top = n_layers - 1
        h, a, tok_ = fwd_up(meta, xc, ups[0], 0, deps=(tok_,))
        x, tok_ = fwd_down(meta, xc, a, downs[0], 0, deps=(tok_,))
        xs, hs, acts = [xc, x], [h], [a]
        for l in range(1, top):
            if l == 2:
                dxs[n_layers], tok_ = pack(meta, dy_own, dy_gots, True, deps=(tok_,))
            h, a, x, tok_ = fwd_layer(meta, xs[-1], ups[l], downs[l], l, deps=(tok_,))
            xs.append(x)
            hs.append(h)
            acts.append(a)
        h, a, *parts, tok_ = fwd_up(
            meta, xs[-1], ups[top], top, dy=dxs[n_layers], n_p=pieces_of("d", top), deps=(tok_,)
        )
        hs.append(h)
        acts.append(a)
        shares = {("d", top, p): swap(v) for p, v in enumerate(parts)}

        dhs, moved, sums = {}, {}, {}
        bufs = {"d": None, "u": None}
        shapes = {"d": (n_layers, unit_f, d), "u": (n_layers, unit_d, f)}
        for what, *key in ORDER:
            key = tuple(key)
            if what == "B1":
                l, part = key
                dhs[key], out, tok_ = bwd_hidden(
                    meta, dxs[l + 1], hs[l], xs[l], downs[l], l, part, 2, deps=(tok_,)
                )
            elif what == "dx":
                l = key[0]
                dh = (dhs[l, 0], dhs[l, 1])
                dxs[l], out, tok_ = bwd_input(meta, dxs[l + 1], dh, acts[l - 1], ups[l], l, deps=(tok_,))
            elif what == "PUT":
                kind, l, p = key
                row = p * unit_f // pieces_of(kind, l) if kind == "d" else 0
                col = 0 if kind == "d" else p * f // pieces_of(kind, l)
                bufs[kind], tok_ = finish(meta, bufs[kind], *sums[key], shapes[kind], l, row, col, deps=(tok_,))
            else:
                kind, l, p = key
                n_p = pieces_of(kind, l)
                if kind == "d":
                    v, g, at = acts[l], dxs[l + 1], (p, n_p)
                    share = shares.get(key, shares.get(key[:2]))
                else:
                    part, n_p = p * 2 // n_p, n_p // 2
                    v, g, at, share = xs[l], dhs[l, part], (p % n_p, n_p), shares[kind, l, part]
                out, tok_ = grad(meta, kind, what, v, g, *at, share, moved[key] if what == "K" else None, deps=(tok_,))
            if what == "B1":
                shares["u", *key] = swap(out)
            elif what == "dx":
                shares["d", l - 1] = swap(out)
            elif what == "S":
                moved[key] = lax.ppermute(out, "fsdp", SWAP_X)
            elif what == "K":
                sums[key] = (out, swap_y(out))

        return bufs["u"], bufs["d"]

    return jax.shard_map(
        device_grads, mesh=mesh, in_specs=(tok_spec, tok_spec, len_spec, w_spec, w_spec),
        out_specs=(w_spec, w_spec), check_vma=False,
    )
```

profile of v0, /device:TPU:0, one launch (start us, length us, event | category | flops | bytes accessed | tf_op | source)
XLA Modules:
  0.0 2119.9 jit_solution(6762007547818818475)
XLA Ops:
  32.6 20.4 collective-permute-done.23.refs_3_.refs_7_
  56.2 19.2 collective-permute-done.17.refs_3_.refs_7_
  86.3 21.3 %collective-permute-done.5.refs_3_ = bf16[2,256,1024]{2,1,0:T(8,128)(2,1)S(1)} collective-permute-done((bf16[2,256,1024]{2,1,0:T(8,128)(2,1)}, bf16[2,256,1024]{2,1,0:T(8,128)(2,1)S(1)}, u32[]{:S(2)}, u32[]{:S(2)}) %collective-permute-start.5) | collective-permute-done | bytes 1048608 | tf_op jit(solution)/shard_map/ppermute | solution.py:672
  111.7 11.4 collective-permute-done.10.refs_3_
  147.4 12.4 collective-permute-done.8.refs_3_
  160.1 21.4 %collective-permute-done.14.refs_5_.refs_7_ = bf16[512,1024]{1,0:T(8,128)(2,1)} collective-permute-done((bf16[512,1024]{1,0:T(8,128)(2,1)}, bf16[512,1024]{1,0:T(8,128)(2,1)}, u32[]{:S(2)}, u32[]{:S(2)}) %collective-permute-start.14) | collective-permute-done | bytes 1048608 | tf_op jit(solution)/shard_map/ppermute | solution.py:643
  183.1 43.7 %shard_map.71 = (bf16[4096,4096]{1,0:T(8,128)(2,1)}, bf16[4096,4096]{1,0:T(8,128)(2,1)}, f32[8,128]{1,0:T(8,128)}) custom-call(s32[16]{0:T(128)} %stack.29.meta, bf16[4096,1024]{1,0:T(8,128)(2,1)} %get-tuple-element.165.refs_0_.refs_2_.refs_3_, bf16[4,256,4096]{2,1,0:T(8,128)(2,1)} %refs_5_.5, bf16[4,256,4096]{2,1,0:T(8,128)(2,1)} %collective-permute-done.9.refs_2_.refs_6_, ...), custom_call_target="tpu_custom_call" | custom-call | flops 30064771072 | bytes 66060288 | tf_op jit(solution)/shard_map/pallas_call | solution.py:80
  228.9 34.0 %shard_map.72 = (bf16[4096,1024]{1,0:T(8,128)(2,1)}, f32[8,128]{1,0:T(8,128)}) custom-call(s32[16]{0:T(128)} %stack.29.meta, bf16[4096,1024]{1,0:T(8,128)(2,1)} %get-tuple-element.165.refs_0_.refs_2_.refs_3_, bf16[4096,4096]{1,0:T(8,128)(2,1)} %get-tuple-element.170.refs_1_.refs_3_.refs_4_.refs_0_, bf16[4,1024,1024]{2,1,0:T(8,128)(2,1)} %refs_4_.15, ...), custom_call_target="tpu_custom_call" | custom-call | flops 30064771072 | bytes 44040192 | tf_op jit(solution)/shard_map/pallas_call | solution.py:80
  263.0 12.6 collective-permute-done.27.refs_9_.refs_6_
  276.1 62.2 %shard_map.73 = (bf16[4096,4096]{1,0:T(8,128)(2,1)}, bf16[4096,4096]{1,0:T(8,128)(2,1)}, bf16[4096,1024]{1,0:T(8,128)(2,1)}, f32[8,128]{1,0:T(8,128)}) custom-call(s32[16]{0:T(128)} %stack.29.meta, bf16[4096,1024]{1,0:T(8,128)(2,1)} %get-tuple-element.172.refs_0_.refs_2_.refs_3_, bf16[4,256,4096]{2,1,0:T(8,128)(2,1)} %refs_5_.5, ...), custom_call_target="tpu_custom_call" | custom-call | flops 60129542144 | bytes 73400320 | tf_op jit(solution)/shard_map/pallas_call | solution.py:80
  345.6 62.2 %shard_map.75 = (bf16[4096,4096]{1,0:T(8,128)(2,1)}, bf16[4096,4096]{1,0:T(8,128)(2,1)}, bf16[4096,1024]{1,0:T(8,128)(2,1)}, f32[8,128]{1,0:T(8,128)}) custom-call(s32[16]{0:T(128)} %stack.29.meta, bf16[4096,1024]{1,0:T(8,128)(2,1)} %get-tuple-element.176.refs_0_.refs_2_.refs_3_, bf16[4,256,4096]{2,1,0:T(8,128)(2,1)} %refs_5_.5, ...), custom_call_target="tpu_custom_call" | custom-call | flops 60129542144 | bytes 73400320 | tf_op jit(solution)/shard_map/pallas_call | solution.py:80
  407.9 60.5 %shard_map.76 = (bf16[4096,4096]{1,0:T(8,128)(2,1)}, bf16[4096,4096]{1,0:T(8,128)(2,1)}, f32[2,512,1024]{2,1,0:T(8,128)}, f32[2,512,1024]{2,1,0:T(8,128)}, f32[8,128]{1,0:T(8,128)}) custom-call(s32[16]{0:T(128)} %stack.29.meta, bf16[4096,1024]{1,0:T(8,128)(2,1)} %get-tuple-element.178.refs_0_.refs_2_.refs_3_, bf16[4,256,4096]{2,1,0:T(8,128)(2,1)} %refs_5_.5, ...), custom_call_target="tpu_custom_call" | custom-call | flops 45097156608 | bytes 66060288 | tf_op jit(solution)/shard_map/pallas_call | solution.py:80
  468.8 47.9 %collective-permute-done.31.refs_6_ = bf16[1024,1024]{1,0:T(8,128)(2,1)} collective-permute-done((bf16[1024,1024]{1,0:T(8,128)(2,1)}, bf16[1024,1024]{1,0:T(8,128)(2,1)}, u32[]{:S(2)}, u32[]{:S(2)}) %collective-permute-start.31) | collective-permute-done | bytes 2097184 | tf_op jit(solution)/shard_map/ppermute | solution.py:655
  525.5 37.0 %shard_map.78 = (bf16[4096,2048]{1,0:T(8,128)(2,1)}, f32[2,256,2048]{2,1,0:T(8,128)}, f32[8,128]{1,0:T(8,128)}) custom-call(s32[16]{0:T(128)} %stack.29.meta, bf16[4096,1024]{1,0:T(8,128)(2,1)} %get-tuple-element.175.refs_5_.refs_1_.refs_0_, bf16[4096,4096]{1,0:T(8,128)(2,1)} %get-tuple-element.180.refs_1_, ...), custom_call_target="tpu_custom_call" | custom-call | flops 22548578304 | bytes 36700160 | tf_op jit(solution)/shard_map/pallas_call | solution.py:80
  579.0 37.0 %shard_map.81 = (bf16[4096,2048]{1,0:T(8,128)(2,1)}, f32[2,256,2048]{2,1,0:T(8,128)}, f32[8,128]{1,0:T(8,128)}) custom-call(s32[16]{0:T(128)} %stack.29.meta, bf16[4096,1024]{1,0:T(8,128)(2,1)} %get-tuple-element.175.refs_5_.refs_1_.refs_0_, bf16[4096,4096]{1,0:T(8,128)(2,1)} %get-tuple-element.180.refs_1_, ...), custom_call_target="tpu_custom_call" | custom-call | flops 22548578304 | bytes 36700160 | tf_op jit(solution)/shard_map/pallas_call | solution.py:80
  627.0 50.9 %shard_map.83 = (bf16[4096,1024]{1,0:T(8,128)(2,1)}, f32[2,1024,1024]{2,1,0:T(8,128)}, f32[8,128]{1,0:T(8,128)}) custom-call(s32[16]{0:T(128)} %stack.29.meta, bf16[4096,1024]{1,0:T(8,128)(2,1)} %get-tuple-element.175.refs_5_.refs_1_.refs_0_, bf16[4096,2048]{1,0:T(8,128)(2,1)} %get-tuple-element.191.refs_1_, ...), custom_call_target="tpu_custom_call" | custom-call | flops 45097156608 | bytes 44040192 | tf_op jit(solution)/shard_map/pallas_call | solution.py:80
  680.5 17.0 collective-permute-done.37.refs_2_
  706.1 21.2 collective-permute-done.41.refs_3_
  736.0 36.2 %collective-permute-done.40.refs_3_ = f32[256,2048]{1,0:T(8,128)} collective-permute-done((f32[256,2048]{1,0:T(8,128)}, f32[256,2048]{1,0:T(8,128)}, u32[]{:S(2)}, u32[]{:S(2)}) %collective-permute-start.40) | collective-permute-done | bytes 2097184 | tf_op jit(solution)/shard_map/ppermute | solution.py:749
  781.5 11.3 shard_map.87
  792.8 36.9 %shard_map.88 = (bf16[4096,2048]{1,0:T(8,128)(2,1)}, f32[2,256,2048]{2,1,0:T(8,128)}, f32[8,128]{1,0:T(8,128)}) custom-call(s32[16]{0:T(128)} %stack.29.meta, bf16[4096,1024]{1,0:T(8,128)(2,1)} %get-tuple-element.196.refs_1_.refs_0_, bf16[4096,4096]{1,0:T(8,128)(2,1)} %get-tuple-element.197.refs_1_, ...), custom_call_target="tpu_custom_call" | custom-call | flops 22548578304 | bytes 36700160 | tf_op jit(solution)/shard_map/pallas_call | solution.py:80
  829.8 9.3 shard_map.89
  839.1 37.0 %shard_map.90 = (bf16[4096,2048]{1,0:T(8,128)(2,1)}, f32[2,256,2048]{2,1,0:T(8,128)}, f32[8,128]{1,0:T(8,128)}) custom-call(s32[16]{0:T(128)} %stack.29.meta, bf16[4096,1024]{1,0:T(8,128)(2,1)} %get-tuple-element.196.refs_1_.refs_0_, bf16[4096,4096]{1,0:T(8,128)(2,1)} %get-tuple-element.197.refs_1_, ...), custom_call_target="tpu_custom_call" | custom-call | flops 22548578304 | bytes 36700160 | tf_op jit(solution)/shard_map/pallas_call | solution.py:80
  894.0 75.6 %collective-permute-done.42.refs_3_ = f32[1024,1024]{1,0:T(8,128)} collective-permute-done((f32[1024,1024]{1,0:T(8,128)}, f32[1024,1024]{1,0:T(8,128)}, u32[]{:S(2)}, u32[]{:S(2)}) %collective-permute-start.42) | collective-permute-done | bytes 4194336 | tf_op jit(solution)/shard_map/ppermute | solution.py:749
  969.5 12.1 shard_map.93
  981.6 50.8 %shard_map.94 = (bf16[4096,1024]{1,0:T(8,128)(2,1)}, f32[2,1024,1024]{2,1,0:T(8,128)}, f32[8,128]{1,0:T(8,128)}) custom-call(s32[16]{0:T(128)} %stack.29.meta, bf16[4096,1024]{1,0:T(8,128)(2,1)} %get-tuple-element.196.refs_1_.refs_0_, bf16[4096,2048]{1,0:T(8,128)(2,1)} %get-tuple-element.210.refs_1_, bf16[4096,2048]{1,0:T(8,128)(2,1)} %get-tuple-element.211.refs_1_.refs_2_, ...), custom_call_target="tpu_custom_call" | custom-call | flops 45097156608 | bytes 44040192 | tf_op jit(solution)/shard_map/pallas_call | solution.py:80
  1034.5 46.8 %collective-permute-done.46.refs_3_ = f32[256,2048]{1,0:T(8,128)} collective-permute-done((f32[256,2048]{1,0:T(8,128)}, f32[256,2048]{1,0:T(8,128)}, u32[]{:S(2)}, u32[]{:S(2)}) %collective-permute-start.46) | collective-permute-done | bytes 2097184 | tf_op jit(solution)/shard_map/ppermute | solution.py:749
  1081.3 9.7 shard_map.95
  1091.0 11.3 shard_map.96
  1102.4 37.1 %shard_map.97 = (bf16[4096,2048]{1,0:T(8,128)(2,1)}, f32[2,256,2048]{2,1,0:T(8,128)}, f32[8,128]{1,0:T(8,128)}) custom-call(s32[16]{0:T(128)} %stack.29.meta, bf16[4096,1024]{1,0:T(8,128)(2,1)} %get-tuple-element.220.refs_1_.refs_0_, bf16[4096,4096]{1,0:T(8,128)(2,1)} %get-tuple-element.221.refs_1_, ...), custom_call_target="tpu_custom_call" | custom-call | flops 22548578304 | bytes 36700160 | tf_op jit(solution)/shard_map/pallas_call | solution.py:80
  1139.5 9.4 shard_map.98
  1148.9 37.0 %shard_map.99 = (bf16[4096,2048]{1,0:T(8,128)(2,1)}, f32[2,256,2048]{2,1,0:T(8,128)}, f32[8,128]{1,0:T(8,128)}) custom-call(s32[16]{0:T(128)} %stack.29.meta, bf16[4096,1024]{1,0:T(8,128)(2,1)} %get-tuple-element.220.refs_1_.refs_0_, bf16[4096,4096]{1,0:T(8,128)(2,1)} %get-tuple-element.221.refs_1_, ...), custom_call_target="tpu_custom_call" | custom-call | flops 22548578304 | bytes 36700160 | tf_op jit(solution)/shard_map/pallas_call | solution.py:80
  1186.5 29.1 %collective-permute-done.50.refs_3_ = f32[1024,1024]{1,0:T(8,128)} collective-permute-done((f32[1024,1024]{1,0:T(8,128)}, f32[1024,1024]{1,0:T(8,128)}, u32[]{:S(2)}, u32[]{:S(2)}) %collective-permute-start.50) | collective-permute-done | bytes 4194336 | tf_op jit(solution)/shard_map/ppermute | solution.py:749
  1215.7 11.9 shard_map.100
  1244.8 50.9 %shard_map.103 = (bf16[4096,1024]{1,0:T(8,128)(2,1)}, f32[2,1024,1024]{2,1,0:T(8,128)}, f32[8,128]{1,0:T(8,128)}) custom-call(s32[16]{0:T(128)} %stack.29.meta, bf16[4096,1024]{1,0:T(8,128)(2,1)} %get-tuple-element.220.refs_1_.refs_0_, bf16[4096,2048]{1,0:T(8,128)(2,1)} %get-tuple-element.227.refs_1_, bf16[4096,2048]{1,0:T(8,128)(2,1)} %get-tuple-element.231.refs_1_.refs_2_, ...), custom_call_target="tpu_custom_call" | custom-call | flops 45097156608 | bytes 44040192 | tf_op jit(solution)/shard_map/pallas_call | solution.py:80
  1299.8 44.8 %collective-permute-done.53.refs_3_ = f32[256,2048]{1,0:T(8,128)} collective-permute-done((f32[256,2048]{1,0:T(8,128)}, f32[256,2048]{1,0:T(8,128)}, u32[]{:S(2)}, u32[]{:S(2)}) %collective-permute-start.53) | collective-permute-done | bytes 2097184 | tf_op jit(solution)/shard_map/ppermute | solution.py:749
  1369.6 19.9 collective-permute-done.51.refs_3_
  1398.8 36.8 %shard_map.108 = (bf16[4096,2048]{1,0:T(8,128)(2,1)}, f32[2,256,2048]{2,1,0:T(8,128)}, f32[8,128]{1,0:T(8,128)}) custom-call(s32[16]{0:T(128)} %stack.29.meta, bf16[4096,1024]{1,0:T(8,128)(2,1)} %get-tuple-element.239.refs_1_.refs_0_, bf16[4096,4096]{1,0:T(8,128)(2,1)} %get-tuple-element.240.refs_1_, ...), custom_call_target="tpu_custom_call" | custom-call | flops 22548578304 | bytes 36700160 | tf_op jit(solution)/shard_map/pallas_call | solution.py:80
  1444.1 36.9 %shard_map.110 = (bf16[4096,2048]{1,0:T(8,128)(2,1)}, f32[2,256,2048]{2,1,0:T(8,128)}, f32[8,128]{1,0:T(8,128)}) custom-call(s32[16]{0:T(128)} %stack.29.meta, bf16[4096,1024]{1,0:T(8,128)(2,1)} %get-tuple-element.239.refs_1_.refs_0_, bf16[4096,4096]{1,0:T(8,128)(2,1)} %get-tuple-element.240.refs_1_, ...), custom_call_target="tpu_custom_call" | custom-call | flops 22548578304 | bytes 36700160 | tf_op jit(solution)/shard_map/pallas_call | solution.py:80
  1483.2 136.1 %collective-permute-done.69.refs_1_ = f32[512,1024]{1,0:T(8,128)} collective-permute-done((f32[512,1024]{1,0:T(8,128)}, f32[512,1024]{1,0:T(8,128)}, u32[]{:S(2)}, u32[]{:S(2)}) %collective-permute-start.69) | collective-permute-done | bytes 2097184 | tf_op jit(solution)/shard_map/ppermute | solution.py:643
  1638.0 30.1 %collective-permute-done.63.refs_1_ = f32[256,2048]{1,0:T(8,128)} collective-permute-done((f32[256,2048]{1,0:T(8,128)}, f32[256,2048]{1,0:T(8,128)}, u32[]{:S(2)}, u32[]{:S(2)}) %collective-permute-start.63) | collective-permute-done | bytes 2097184 | tf_op jit(solution)/shard_map/ppermute | solution.py:643
  1675.7 37.4 %collective-permute-done.67.refs_1_ = f32[256,2048]{1,0:T(8,128)} collective-permute-done((f32[256,2048]{1,0:T(8,128)}, f32[256,2048]{1,0:T(8,128)}, u32[]{:S(2)}, u32[]{:S(2)}) %collective-permute-start.67) | collective-permute-done | bytes 2097184 | tf_op jit(solution)/shard_map/ppermute | solution.py:643
  1713.1 44.9 %collective-permute-done.60.refs_1_ = f32[512,1024]{1,0:T(8,128)} collective-permute-done((f32[512,1024]{1,0:T(8,128)}, f32[512,1024]{1,0:T(8,128)}, u32[]{:S(2)}, u32[]{:S(2)}) %collective-permute-start.60) | collective-permute-done | bytes 2097184 | tf_op jit(solution)/shard_map/ppermute | solution.py:643
  1808.6 39.3 %collective-permute-done.70.refs_1_ = f32[512,1024]{1,0:T(8,128)} collective-permute-done((f32[512,1024]{1,0:T(8,128)}, f32[512,1024]{1,0:T(8,128)}, u32[]{:S(2)}, u32[]{:S(2)}) %collective-permute-start.70) | collective-permute-done | bytes 2097184 | tf_op jit(solution)/shard_map/ppermute | solution.py:643
  1849.9 110.3 %collective-permute-done.68.refs_1_ = f32[256,1024]{1,0:T(8,128)} collective-permute-done((f32[256,1024]{1,0:T(8,128)}, f32[256,1024]{1,0:T(8,128)}, u32[]{:S(2)}, u32[]{:S(2)}) %collective-permute-start.68) | collective-permute-done | bytes 1048608 | tf_op jit(solution)/shard_map/ppermute | solution.py:643
  1994.5 78.1 %collective-permute-done.76.refs_1_ = f32[256,1024]{1,0:T(8,128)} collective-permute-done((f32[256,1024]{1,0:T(8,128)}, f32[256,1024]{1,0:T(8,128)}, u32[]{:S(2)}, u32[]{:S(2)}) %collective-permute-start.76) | collective-permute-done | bytes 1048608 | tf_op jit(solution)/shard_map/ppermute | solution.py:643
  2084.8 10.3 collective-permute-done.73.refs_1_
  2104.8 11.4 collective-permute-done.72.refs_1_
  (206 shorter events, 371.6 us)
Async XLA Ops:
  0.6 182.3 %collective-permute-start.9 = (bf16[4,256,4096]{2,1,0:T(8,128)(2,1)}, bf16[4,256,4096]{2,1,0:T(8,128)(2,1)}, u32[]{:S(2)}, u32[]{:S(2)}) collective-permute-start(bf16[4,256,4096]{2,1,0:T(8,128)(2,1)} %refs_5_.5), channel_id=1, source_target_pairs={{0,1},{1,0},{2,3},{3,2},{4,5},{5,4},{6,7},{7,6}} | collective-permute-start | bytes 25165832 | tf_op jit(solution)/shard_map/ppermute | solution.py:640
  17.5 210.9 %collective-permute-start.12 = (bf16[4,1024,1024]{2,1,0:T(8,128)(2,1)}, bf16[4,1024,1024]{2,1,0:T(8,128)(2,1)}, u32[]{:S(2)}, u32[]{:S(2)}) collective-permute-start(bf16[4,1024,1024]{2,1,0:T(8,128)(2,1)} %refs_4_.15), channel_id=1, source_target_pairs={{0,1},{1,0},{2,3},{3,2},{4,5},{5,4},{6,7},{7,6}} | collective-permute-start | bytes 25165832 | tf_op jit(solution)/shard_map/ppermute | solution.py:640
  19.6 55.8 %collective-permute-start.17 = (bf16[128,4096]{1,0:T(8,128)(2,1)}, bf16[128,4096]{1,0:T(8,128)(2,1)}, u32[]{:S(2)}, u32[]{:S(2)}) collective-permute-start(bf16[128,4096]{1,0:T(8,128)(2,1)} %get-tuple-element.322), channel_id=1, source_target_pairs={{0,2},{2,0},{1,3},{3,1},{4,6},{6,4},{5,7},{7,5}} | collective-permute-start | bytes 3145736 | tf_op jit(solution)/shard_map/ppermute | solution.py:655
  30.6 51.5 %collective-permute-start.4 = (bf16[2,256,1024]{2,1,0:T(8,128)(2,1)}, bf16[2,256,1024]{2,1,0:T(8,128)(2,1)}, u32[]{:S(2)}, u32[]{:S(2)}) collective-permute-start(bf16[2,256,1024]{2,1,0:T(8,128)(2,1)} %get-tuple-element.161), channel_id=1, source_target_pairs={{0,4},{1,5},{2,6},{3,7},{4,0},{5,1},{6,2},{7,3}} | collective-permute-start | bytes 3145736 | tf_op jit(solution)/shard_map/ppermute | solution.py:672
  53.1 81.0 %collective-permute-start.3 = (bf16[2,768,1024]{2,1,0:T(8,128)(2,1)}, bf16[2,768,1024]{2,1,0:T(8,128)(2,1)}, u32[]{:S(2)}, u32[]{:S(2)}) collective-permute-start(bf16[2,768,1024]{2,1,0:T(8,128)(2,1)} %get-tuple-element.160), channel_id=1, source_target_pairs={{0,1},{1,0},{2,3},{3,2},{4,5},{5,4},{6,7},{7,6}} | collective-permute-start | bytes 9437192 | tf_op jit(solution)/shard_map/ppermute | solution.py:672
  123.1 58.9 %collective-permute-start.11 = (bf16[256,4096]{1,0:T(8,128)(2,1)}, bf16[256,4096]{1,0:T(8,128)(2,1)}, u32[]{:S(2)}, u32[]{:S(2)}) collective-permute-start(bf16[256,4096]{1,0:T(8,128)(2,1)} %collective-permute-done.10.refs_3_), channel_id=1, source_target_pairs={{0,1},{1,0},{2,3},{3,2},{4,5},{5,4},{6,7},{7,6}} | collective-permute-start | bytes 6291464 | tf_op jit(solution)/shard_map/ppermute | solution.py:640
  159.8 67.4 %collective-permute-start.21 = (bf16[1024,1024]{1,0:T(8,128)(2,1)}, bf16[1024,1024]{1,0:T(8,128)(2,1)}, u32[]{:S(2)}, u32[]{:S(2)}) collective-permute-start(bf16[1024,1024]{1,0:T(8,128)(2,1)} %get-tuple-element.320), channel_id=1, source_target_pairs={{0,2},{2,0},{1,3},{3,1},{4,6},{6,4},{5,7},{7,5}} | collective-permute-start | bytes 6291464 | tf_op jit(solution)/shard_map/ppermute | solution.py:655
  262.9 75.4 %collective-permute-start.29 = (bf16[256,4096]{1,0:T(8,128)(2,1)}, bf16[256,4096]{1,0:T(8,128)(2,1)}, u32[]{:S(2)}, u32[]{:S(2)}) collective-permute-start(bf16[256,4096]{1,0:T(8,128)(2,1)} %slice_bitcast_fusion.1), channel_id=1, source_target_pairs={{0,2},{2,0},{1,3},{3,1},{4,6},{6,4},{5,7},{7,5}} | collective-permute-start | bytes 6291464 | tf_op jit(solution)/shard_map/ppermute | solution.py:655
  263.0 75.9 %collective-permute-start.6 = (bf16[2,768,1024]{2,1,0:T(8,128)(2,1)}, bf16[2,768,1024]{2,1,0:T(8,128)(2,1)}, u32[]{:S(2)}, u32[]{:S(2)}) collective-permute-start(bf16[2,768,1024]{2,1,0:T(8,128)(2,1)} %get-tuple-element.166), channel_id=1, source_target_pairs={{0,1},{1,0},{2,3},{3,2},{4,5},{5,4},{6,7},{7,6}} | collective-permute-start | bytes 9437192 | tf_op jit(solution)/shard_map/ppermute | solution.py:672
  275.6 70.0 %collective-permute-start.25 = (bf16[128,4096]{1,0:T(8,128)(2,1)}, bf16[128,4096]{1,0:T(8,128)(2,1)}, u32[]{:S(2)}, u32[]{:S(2)}) collective-permute-start(bf16[128,4096]{1,0:T(8,128)(2,1)} %collective-permute-done.23.refs_3_.refs_7_), channel_id=1, source_target_pairs={{0,1},{1,0},{2,3},{3,2},{4,5},{5,4},{6,7},{7,6}} | collective-permute-start | bytes 3145736 | tf_op jit(solution)/shard_map/ppermute | solution.py:640
  275.6 70.0 %collective-permute-start.26 = (bf16[128,4096]{1,0:T(8,128)(2,1)}, bf16[128,4096]{1,0:T(8,128)(2,1)}, u32[]{:S(2)}, u32[]{:S(2)}) collective-permute-start(bf16[128,4096]{1,0:T(8,128)(2,1)} %collective-permute-done.24.refs_4_.refs_8_), channel_id=1, source_target_pairs={{0,1},{1,0},{2,3},{3,2},{4,5},{5,4},{6,7},{7,6}} | collective-permute-start | bytes 3145736 | tf_op jit(solution)/shard_map/ppermute | solution.py:640
  276.1 69.5 %collective-permute-start.28 = (bf16[1024,1024]{1,0:T(8,128)(2,1)}, bf16[1024,1024]{1,0:T(8,128)(2,1)}, u32[]{:S(2)}, u32[]{:S(2)}) collective-permute-start(bf16[1024,1024]{1,0:T(8,128)(2,1)} %collective-permute-done.27.refs_9_.refs_6_), channel_id=1, source_target_pairs={{0,1},{1,0},{2,3},{3,2},{4,5},{5,4},{6,7},{7,6}} | collective-permute-start | bytes 6291464 | tf_op jit(solution)/shard_map/ppermute | solution.py:640
  338.3 69.5 %collective-permute-start.30 = (bf16[256,4096]{1,0:T(8,128)(2,1)}, bf16[256,4096]{1,0:T(8,128)(2,1)}, u32[]{:S(2)}, u32[]{:S(2)}) collective-permute-start(bf16[256,4096]{1,0:T(8,128)(2,1)} %collective-permute-done.29.refs_3_.refs_7_), channel_id=1, source_target_pairs={{0,1},{1,0},{2,3},{3,2},{4,5},{5,4},{6,7},{7,6}} | collective-permute-start | bytes 6291464 | tf_op jit(solution)/shard_map/ppermute | solution.py:640
  468.4 48.9 %collective-permute-start.33 = (f32[2,512,1024]{2,1,0:T(8,128)}, f32[2,512,1024]{2,1,0:T(8,128)}, u32[]{:S(2)}, u32[]{:S(2)}) collective-permute-start(f32[2,512,1024]{2,1,0:T(8,128)} %get-tuple-element.182), channel_id=1, source_target_pairs={{0,1},{1,0},{2,3},{3,2},{4,5},{5,4},{6,7},{7,6}} | collective-permute-start | bytes 12582920 | tf_op jit(solution)/shard_map/ppermute | solution.py:640
  677.9 103.6 %collective-permute-start.39 = (f32[2,1024,1024]{2,1,0:T(8,128)}, f32[2,1024,1024]{2,1,0:T(8,128)}, u32[]{:S(2)}, u32[]{:S(2)}) collective-permute-start(f32[2,1024,1024]{2,1,0:T(8,128)} %get-tuple-element.201), channel_id=1, source_target_pairs={{0,1},{1,0},{2,3},{3,2},{4,5},{5,4},{6,7},{7,6}} | collective-permute-start | bytes 25165832 | tf_op jit(solution)/shard_map/ppermute | solution.py:640
  678.5 93.8 %collective-permute-start.40 = (f32[256,2048]{1,0:T(8,128)}, f32[256,2048]{1,0:T(8,128)}, u32[]{:S(2)}, u32[]{:S(2)}) collective-permute-start(f32[256,2048]{1,0:T(8,128)} %get-tuple-element.202), channel_id=1, source_target_pairs={{0,2},{2,0},{1,3},{3,1},{4,6},{6,4},{5,7},{7,5}} | collective-permute-start | bytes 6291464 | tf_op jit(solution)/shard_map/ppermute | solution.py:749
  706.1 123.8 %collective-permute-start.38 = (f32[256,2048]{1,0:T(8,128)}, f32[256,2048]{1,0:T(8,128)}, u32[]{:S(2)}, u32[]{:S(2)}) collective-permute-start(f32[256,2048]{1,0:T(8,128)} %get-tuple-element.200), channel_id=1, source_target_pairs={{0,2},{2,0},{1,3},{3,1},{4,6},{6,4},{5,7},{7,5}} | collective-permute-start | bytes 6291464 | tf_op jit(solution)/shard_map/ppermute | solution.py:749
  876.7 92.8 %collective-permute-start.42 = (f32[1024,1024]{1,0:T(8,128)}, f32[1024,1024]{1,0:T(8,128)}, u32[]{:S(2)}, u32[]{:S(2)}) collective-permute-start(f32[1024,1024]{1,0:T(8,128)} %get-tuple-element.213), channel_id=1, source_target_pairs={{0,2},{2,0},{1,3},{3,1},{4,6},{6,4},{5,7},{7,5}} | collective-permute-start | bytes 12582920 | tf_op jit(solution)/shard_map/ppermute | solution.py:749
  1032.5 58.6 %collective-permute-start.45 = (f32[2,1024,1024]{2,1,0:T(8,128)}, f32[2,1024,1024]{2,1,0:T(8,128)}, u32[]{:S(2)}, u32[]{:S(2)}) collective-permute-start(f32[2,1024,1024]{2,1,0:T(8,128)} %get-tuple-element.222), channel_id=1, source_target_pairs={{0,1},{1,0},{2,3},{3,2},{4,5},{5,4},{6,7},{7,6}} | collective-permute-start | bytes 25165832 | tf_op jit(solution)/shard_map/ppermute | solution.py:640
  1032.5 48.8 %collective-permute-start.46 = (f32[256,2048]{1,0:T(8,128)}, f32[256,2048]{1,0:T(8,128)}, u32[]{:S(2)}, u32[]{:S(2)}) collective-permute-start(f32[256,2048]{1,0:T(8,128)} %get-tuple-element.223), channel_id=1, source_target_pairs={{0,2},{2,0},{1,3},{3,1},{4,6},{6,4},{5,7},{7,5}} | collective-permute-start | bytes 6291464 | tf_op jit(solution)/shard_map/ppermute | solution.py:749
  1032.5 107.0 %collective-permute-start.47 = (f32[256,2048]{1,0:T(8,128)}, f32[256,2048]{1,0:T(8,128)}, u32[]{:S(2)}, u32[]{:S(2)}) collective-permute-start(f32[256,2048]{1,0:T(8,128)} %get-tuple-element.228), channel_id=1, source_target_pairs={{0,2},{2,0},{1,3},{3,1},{4,6},{6,4},{5,7},{7,5}} | collective-permute-start | bytes 6291464 | tf_op jit(solution)/shard_map/ppermute | solution.py:749
  1102.4 113.3 %collective-permute-start.50 = (f32[1024,1024]{1,0:T(8,128)}, f32[1024,1024]{1,0:T(8,128)}, u32[]{:S(2)}, u32[]{:S(2)}) collective-permute-start(f32[1024,1024]{1,0:T(8,128)} %get-tuple-element.234), channel_id=1, source_target_pairs={{0,2},{2,0},{1,3},{3,1},{4,6},{6,4},{5,7},{7,5}} | collective-permute-start | bytes 12582920 | tf_op jit(solution)/shard_map/ppermute | solution.py:749
  1186.0 50.1 %collective-permute-start.48 = (f32[2,256,2048]{2,1,0:T(8,128)}, f32[2,256,2048]{2,1,0:T(8,128)}, u32[]{:S(2)}, u32[]{:S(2)}) collective-permute-start(f32[2,256,2048]{2,1,0:T(8,128)} %get-tuple-element.232), channel_id=1, source_target_pairs={{0,1},{1,0},{2,3},{3,2},{4,5},{5,4},{6,7},{7,6}} | collective-permute-start | bytes 12582920 | tf_op jit(solution)/shard_map/ppermute | solution.py:640
  1295.7 58.2 %collective-permute-start.52 = (f32[2,1024,1024]{2,1,0:T(8,128)}, f32[2,1024,1024]{2,1,0:T(8,128)}, u32[]{:S(2)}, u32[]{:S(2)}) collective-permute-start(f32[2,1024,1024]{2,1,0:T(8,128)} %get-tuple-element.242), channel_id=1, source_target_pairs={{0,1},{1,0},{2,3},{3,2},{4,5},{5,4},{6,7},{7,6}} | collective-permute-start | bytes 25165832 | tf_op jit(solution)/shard_map/ppermute | solution.py:640
  1295.7 48.8 %collective-permute-start.53 = (f32[256,2048]{1,0:T(8,128)}, f32[256,2048]{1,0:T(8,128)}, u32[]{:S(2)}, u32[]{:S(2)}) collective-permute-start(f32[256,2048]{1,0:T(8,128)} %get-tuple-element.243), channel_id=1, source_target_pairs={{0,2},{2,0},{1,3},{3,1},{4,6},{6,4},{5,7},{7,5}} | collective-permute-start | bytes 6291464 | tf_op jit(solution)/shard_map/ppermute | solution.py:749
  1295.8 93.7 %collective-permute-start.51 = (f32[256,2048]{1,0:T(8,128)}, f32[256,2048]{1,0:T(8,128)}, u32[]{:S(2)}, u32[]{:S(2)}) collective-permute-start(f32[256,2048]{1,0:T(8,128)} %get-tuple-element.241), channel_id=1, source_target_pairs={{0,2},{2,0},{1,3},{3,1},{4,6},{6,4},{5,7},{7,5}} | collective-permute-start | bytes 6291464 | tf_op jit(solution)/shard_map/ppermute | solution.py:749
  1297.8 185.4 %collective-permute-start.61 = (f32[512,1024]{1,0:T(8,128)}, f32[512,1024]{1,0:T(8,128)}, u32[]{:S(2)}, u32[]{:S(2)}) collective-permute-start(f32[512,1024]{1,0:T(8,128)} %get-tuple-element.263.refs_0_), channel_id=1, source_target_pairs={{0,4},{4,0},{1,5},{5,1},{2,6},{6,2},{3,7},{7,3}} | collective-permute-start | bytes 6291464 | tf_op jit(solution)/shard_map/ppermute | solution.py:643
  1298.8 184.3 %collective-permute-start.62 = (f32[256,2048]{1,0:T(8,128)}, f32[256,2048]{1,0:T(8,128)}, u32[]{:S(2)}, u32[]{:S(2)}) collective-permute-start(f32[256,2048]{1,0:T(8,128)} %get-tuple-element.264.refs_0_), channel_id=1, source_target_pairs={{0,4},{4,0},{1,5},{5,1},{2,6},{6,2},{3,7},{7,3}} | collective-permute-start | bytes 6291464 | tf_op jit(solution)/shard_map/ppermute | solution.py:643
  1361.8 73.7 %collective-permute-start.55 = (f32[512,1024]{1,0:T(8,128)}, f32[512,1024]{1,0:T(8,128)}, u32[]{:S(2)}, u32[]{:S(2)}) collective-permute-start(f32[512,1024]{1,0:T(8,128)} %get-tuple-element.251), channel_id=1, source_target_pairs={{0,2},{2,0},{1,3},{3,1},{4,6},{6,4},{5,7},{7,5}} | collective-permute-start | bytes 6291464 | tf_op jit(solution)/shard_map/ppermute | solution.py:749
  1481.1 140.3 %collective-permute-start.56 = (f32[2,256,2048]{2,1,0:T(8,128)}, f32[2,256,2048]{2,1,0:T(8,128)}, u32[]{:S(2)}, u32[]{:S(2)}) collective-permute-start(f32[2,256,2048]{2,1,0:T(8,128)} %get-tuple-element.255), channel_id=1, source_target_pairs={{0,1},{1,0},{2,3},{3,2},{4,5},{5,4},{6,7},{7,6}} | collective-permute-start | bytes 12582920 | tf_op jit(solution)/shard_map/ppermute | solution.py:640
  1481.1 155.9 %collective-permute-start.59 = (f32[1024,1024]{1,0:T(8,128)}, f32[1024,1024]{1,0:T(8,128)}, u32[]{:S(2)}, u32[]{:S(2)}) collective-permute-start(f32[1024,1024]{1,0:T(8,128)} %get-tuple-element.261.refs_0_), channel_id=1, source_target_pairs={{0,4},{4,0},{1,5},{5,1},{2,6},{6,2},{3,7},{7,3}} | collective-permute-start | bytes 12582920 | tf_op jit(solution)/shard_map/ppermute | solution.py:643
  1482.2 137.2 %collective-permute-start.69 = (f32[512,1024]{1,0:T(8,128)}, f32[512,1024]{1,0:T(8,128)}, u32[]{:S(2)}, u32[]{:S(2)}) collective-permute-start(f32[512,1024]{1,0:T(8,128)} %get-tuple-element.288.refs_0_), channel_id=1, source_target_pairs={{0,4},{4,0},{1,5},{5,1},{2,6},{6,2},{3,7},{7,3}} | collective-permute-start | bytes 6291464 | tf_op jit(solution)/shard_map/ppermute | solution.py:643
  1483.1 186.0 %collective-permute-start.54 = (f32[2,256,2048]{2,1,0:T(8,128)}, f32[2,256,2048]{2,1,0:T(8,128)}, u32[]{:S(2)}, u32[]{:S(2)}) collective-permute-start(f32[2,256,2048]{2,1,0:T(8,128)} %get-tuple-element.250), channel_id=1, source_target_pairs={{0,1},{1,0},{2,3},{3,2},{4,5},{5,4},{6,7},{7,6}} | collective-permute-start | bytes 12582920 | tf_op jit(solution)/shard_map/ppermute | solution.py:640
  1483.2 137.2 %collective-permute-start.57 = (f32[512,1024]{1,0:T(8,128)}, f32[512,1024]{1,0:T(8,128)}, u32[]{:S(2)}, u32[]{:S(2)}) collective-permute-start(f32[512,1024]{1,0:T(8,128)} %get-tuple-element.256), channel_id=1, source_target_pairs={{0,2},{2,0},{1,3},{3,1},{4,6},{6,4},{5,7},{7,5}} | collective-permute-start | bytes 6291464 | tf_op jit(solution)/shard_map/ppermute | solution.py:749
  1620.4 92.7 %collective-permute-start.67 = (f32[256,2048]{1,0:T(8,128)}, f32[256,2048]{1,0:T(8,128)}, u32[]{:S(2)}, u32[]{:S(2)}) collective-permute-start(f32[256,2048]{1,0:T(8,128)} %get-tuple-element.281.refs_0_), channel_id=1, source_target_pairs={{0,4},{4,0},{1,5},{5,1},{2,6},{6,2},{3,7},{7,3}} | collective-permute-start | bytes 6291464 | tf_op jit(solution)/shard_map/ppermute | solution.py:643
  1621.4 136.7 %collective-permute-start.60 = (f32[512,1024]{1,0:T(8,128)}, f32[512,1024]{1,0:T(8,128)}, u32[]{:S(2)}, u32[]{:S(2)}) collective-permute-start(f32[512,1024]{1,0:T(8,128)} %get-tuple-element.262.refs_0_), channel_id=1, source_target_pairs={{0,4},{4,0},{1,5},{5,1},{2,6},{6,2},{3,7},{7,3}} | collective-permute-start | bytes 6291464 | tf_op jit(solution)/shard_map/ppermute | solution.py:643
  1637.0 171.0 %collective-permute-start.66 = (f32[256,2048]{1,0:T(8,128)}, f32[256,2048]{1,0:T(8,128)}, u32[]{:S(2)}, u32[]{:S(2)}) collective-permute-start(f32[256,2048]{1,0:T(8,128)} %get-tuple-element.280.refs_0_), channel_id=1, source_target_pairs={{0,4},{4,0},{1,5},{5,1},{2,6},{6,2},{3,7},{7,3}} | collective-permute-start | bytes 6291464 | tf_op jit(solution)/shard_map/ppermute | solution.py:643
  1668.1 179.8 %collective-permute-start.70 = (f32[512,1024]{1,0:T(8,128)}, f32[512,1024]{1,0:T(8,128)}, u32[]{:S(2)}, u32[]{:S(2)}) collective-permute-start(f32[512,1024]{1,0:T(8,128)} %get-tuple-element.289.refs_0_), channel_id=1, source_target_pairs={{0,4},{4,0},{1,5},{5,1},{2,6},{6,2},{3,7},{7,3}} | collective-permute-start | bytes 6291464 | tf_op jit(solution)/shard_map/ppermute | solution.py:643
  1669.2 104.0 %collective-permute-start.64 = (f32[256,1024]{1,0:T(8,128)}, f32[256,1024]{1,0:T(8,128)}, u32[]{:S(2)}, u32[]{:S(2)}) collective-permute-start(f32[256,1024]{1,0:T(8,128)} %get-tuple-element.271), channel_id=1, source_target_pairs={{0,2},{2,0},{1,3},{3,1},{4,6},{6,4},{5,7},{7,5}} | collective-permute-start | bytes 3145736 | tf_op jit(solution)/shard_map/ppermute | solution.py:749
  1713.1 66.8 %collective-permute-start.58 = (f32[256,1024]{1,0:T(8,128)}, f32[256,1024]{1,0:T(8,128)}, u32[]{:S(2)}, u32[]{:S(2)}) collective-permute-start(f32[256,1024]{1,0:T(8,128)} %get-tuple-element.260), channel_id=1, source_target_pairs={{0,2},{2,0},{1,3},{3,1},{4,6},{6,4},{5,7},{7,5}} | collective-permute-start | bytes 3145736 | tf_op jit(solution)/shard_map/ppermute | solution.py:749
  1758.0 340.3 %collective-permute-start.77 = (f32[1024,1024]{1,0:T(8,128)}, f32[1024,1024]{1,0:T(8,128)}, u32[]{:S(2)}, u32[]{:S(2)}) collective-permute-start(f32[1024,1024]{1,0:T(8,128)} %get-tuple-element.312.refs_0_), channel_id=1, source_target_pairs={{0,4},{4,0},{1,5},{5,1},{2,6},{6,2},{3,7},{7,3}} | collective-permute-start | bytes 12582920 | tf_op jit(solution)/shard_map/ppermute | solution.py:643
  1773.2 75.7 %collective-permute-start.71 = (f32[256,1024]{1,0:T(8,128)}, f32[256,1024]{1,0:T(8,128)}, u32[]{:S(2)}, u32[]{:S(2)}) collective-permute-start(f32[256,1024]{1,0:T(8,128)} %get-tuple-element.291), channel_id=1, source_target_pairs={{0,2},{2,0},{1,3},{3,1},{4,6},{6,4},{5,7},{7,5}} | collective-permute-start | bytes 3145736 | tf_op jit(solution)/shard_map/ppermute | solution.py:749
  1779.9 180.4 %collective-permute-start.68 = (f32[256,1024]{1,0:T(8,128)}, f32[256,1024]{1,0:T(8,128)}, u32[]{:S(2)}, u32[]{:S(2)}) collective-permute-start(f32[256,1024]{1,0:T(8,128)} %get-tuple-element.282.refs_0_), channel_id=1, source_target_pairs={{0,4},{4,0},{1,5},{5,1},{2,6},{6,2},{3,7},{7,3}} | collective-permute-start | bytes 3145736 | tf_op jit(solution)/shard_map/ppermute | solution.py:643
  1808.0 178.9 %collective-permute-start.65 = (f32[256,1024]{1,0:T(8,128)}, f32[256,1024]{1,0:T(8,128)}, u32[]{:S(2)}, u32[]{:S(2)}) collective-permute-start(f32[256,1024]{1,0:T(8,128)} %get-tuple-element.279), channel_id=1, source_target_pairs={{0,2},{2,0},{1,3},{3,1},{4,6},{6,4},{5,7},{7,5}} | collective-permute-start | bytes 3145736 | tf_op jit(solution)/shard_map/ppermute | solution.py:749
  1847.9 229.0 %collective-permute-start.75 = (f32[256,2048]{1,0:T(8,128)}, f32[256,2048]{1,0:T(8,128)}, u32[]{:S(2)}, u32[]{:S(2)}) collective-permute-start(f32[256,2048]{1,0:T(8,128)} %get-tuple-element.301.refs_0_), channel_id=1, source_target_pairs={{0,4},{4,0},{1,5},{5,1},{2,6},{6,2},{3,7},{7,3}} | collective-permute-start | bytes 6291464 | tf_op jit(solution)/shard_map/ppermute | solution.py:643
  1849.0 231.9 %collective-permute-start.74 = (f32[256,2048]{1,0:T(8,128)}, f32[256,2048]{1,0:T(8,128)}, u32[]{:S(2)}, u32[]{:S(2)}) collective-permute-start(f32[256,2048]{1,0:T(8,128)} %get-tuple-element.300.refs_0_), channel_id=1, source_target_pairs={{0,4},{4,0},{1,5},{5,1},{2,6},{6,2},{3,7},{7,3}} | collective-permute-start | bytes 6291464 | tf_op jit(solution)/shard_map/ppermute | solution.py:643
  1960.3 112.4 %collective-permute-start.76 = (f32[256,1024]{1,0:T(8,128)}, f32[256,1024]{1,0:T(8,128)}, u32[]{:S(2)}, u32[]{:S(2)}) collective-permute-start(f32[256,1024]{1,0:T(8,128)} %get-tuple-element.302.refs_0_), channel_id=1, source_target_pairs={{0,4},{4,0},{1,5},{5,1},{2,6},{6,2},{3,7},{7,3}} | collective-permute-start | bytes 3145736 | tf_op jit(solution)/shard_map/ppermute | solution.py:643
  1986.9 108.2 %collective-permute-start.73 = (f32[256,1024]{1,0:T(8,128)}, f32[256,1024]{1,0:T(8,128)}, u32[]{:S(2)}, u32[]{:S(2)}) collective-permute-start(f32[256,1024]{1,0:T(8,128)} %get-tuple-element.299.refs_0_), channel_id=1, source_target_pairs={{0,4},{4,0},{1,5},{5,1},{2,6},{6,2},{3,7},{7,3}} | collective-permute-start | bytes 3145736 | tf_op jit(solution)/shard_map/ppermute | solution.py:643
  (38 other events, 1116.0 us)
where the time goes:
time: 2130 us; the launch traced here: 2120 us
  Pallas kernels  1070 us (50%)
  waiting for transfers between devices  971 us (46%)
  starting transfers between devices  47.7 us (2%)
  local copies, waits for them, and re-layouts  21.7 us (1%)
    pallas_call x68, Pallas kernels, run(): pl.pallas_call(kern, grid_spec=pltpu.PrefetchScalarGridSpec(num_scalar_pr...  1070 us
    ppermute x19, waiting for transfers between devices, swap_y(): return lax.ppermute(v, 'replica', [(0, 1), (1, 0)])  520 us
    ppermute x16, waiting for transfers between devices, device_grads(): moved[key] = lax.ppermute(out, 'fsdp', SWAP_X)  276 us
    ppermute x8, waiting for transfers between devices, device_grads(): far_x.append(lax.ppermute(src, 'fsdp', SWAP_X))  116 us
  transfers between devices with their start and end apart: 78, of which 30 were waited for; matrix products, arithmetic and copies ran while one was open for 1% of the time, Pallas kernels for 39%

commit v1 on v0

--- a/solution.py
+++ b/solution.py
@@ -606,17 +606,17 @@
 
 PIECES = {("d", 3): 2, ("d", 0): 2, ("u", 0): 4, ("u", 3): 2, ("u", 2): 2, ("u", 1): 2}
 ORDER = [
-    ("S", "d", 3, 0), ("B1", 3, 1), ("S", "d", 3, 1), ("S", "u", 3, 1), ("B1", 3, 0), ("K", "d", 3, 1), ("dx", 3),
-    ("S", "u", 3, 0), ("K", "d", 3, 0), ("K", "u", 3, 1), ("S", "d", 2, 0), ("B1", 2, 1), ("K", "u", 3, 0),
-    ("B1", 2, 0), ("S", "u", 2, 1), ("S", "u", 2, 0), ("K", "d", 2, 0), ("dx", 2), ("K", "u", 2, 1),
-    ("S", "d", 1, 0), ("B1", 1, 0), ("K", "u", 2, 0), ("B1", 1, 1), ("K", "d", 1, 0), ("S", "u", 1, 1),
-    ("S", "u", 1, 0), ("dx", 1), ("K", "u", 1, 1), ("S", "d", 0, 1), ("S", "d", 0, 0), ("K", "u", 1, 0),
-    ("B1", 0, 1), ("K", "d", 0, 1), ("B1", 0, 0), ("K", "d", 0, 0), ("S", "u", 0, 0), ("S", "u", 0, 3),
-    ("S", "u", 0, 1), ("PUT", "u", 3, 1), ("PUT", "d", 3, 1), ("K", "u", 0, 0), ("PUT", "u", 2, 1),
-    ("PUT", "d", 0, 1), ("PUT", "d", 2, 0), ("K", "u", 0, 3), ("S", "u", 0, 2), ("PUT", "u", 0, 0),
-    ("PUT", "u", 1, 1), ("K", "u", 0, 1), ("PUT", "d", 0, 0), ("PUT", "d", 3, 0), ("PUT", "u", 1, 0),
-    ("K", "u", 0, 2), ("PUT", "u", 0, 3), ("PUT", "u", 3, 0), ("PUT", "u", 2, 0), ("PUT", "u", 0, 1),
-    ("PUT", "d", 1, 0), ("PUT", "u", 0, 2),
+    ("S", "d", 3, 0), ("B1", 3, 0), ("S", "d", 3, 1), ("B1", 3, 1), ("S", "u", 3, 0), ("S", "u", 3, 1),
+    ("K", "d", 3, 1), ("dx", 3), ("K", "d", 3, 0), ("K", "u", 3, 0), ("S", "d", 2, 0), ("K", "u", 3, 1),
+    ("B1", 2, 1), ("B1", 2, 0), ("S", "u", 2, 1), ("K", "d", 2, 0), ("S", "u", 2, 0), ("dx", 2), ("K", "u", 2, 1),
+    ("S", "d", 1, 0), ("B1", 1, 1), ("K", "u", 2, 0), ("B1", 1, 0), ("K", "d", 1, 0), ("S", "u", 1, 1),
+    ("S", "u", 1, 0), ("dx", 1), ("PUT", "u", 2, 1), ("K", "u", 1, 1), ("S", "d", 0, 0), ("S", "d", 0, 1),
+    ("K", "u", 1, 0), ("B1", 0, 1), ("K", "d", 0, 0), ("B1", 0, 0), ("K", "d", 0, 1), ("S", "u", 0, 3),
+    ("PUT", "u", 3, 1), ("S", "u", 0, 0), ("PUT", "u", 2, 0), ("PUT", "d", 1, 0), ("S", "u", 0, 2),
+    ("K", "u", 0, 3), ("S", "u", 0, 1), ("PUT", "u", 3, 0), ("K", "u", 0, 0), ("PUT", "u", 1, 1),
+    ("PUT", "u", 1, 0), ("PUT", "d", 0, 1), ("PUT", "d", 2, 0), ("K", "u", 0, 2), ("PUT", "d", 3, 0),
+    ("PUT", "d", 3, 1), ("K", "u", 0, 1), ("PUT", "u", 0, 3), ("PUT", "u", 0, 2), ("PUT", "u", 0, 0),
+    ("PUT", "d", 0, 0), ("PUT", "u", 0, 1),
 ]
 
 

time: 2130 us -> 2020 us (0.948)
  waiting for transfers between devices: 971 us -> 857 us
    ppermute x19, waiting for transfers between devices: 520 us -> 470 us  [swap_y(): return lax.ppermute(v, 'replica', [(0, 1), (1, 0)])]
    ppermute x16, waiting for transfers between devices: 276 us -> 229 us  [device_grads(): moved[key] = lax.ppermute(out, 'fsdp', SWAP_X)]
  transfers between devices with their start and end apart: 78 -> 78, of which waited for: 30 -> 33; matrix products, arithmetic and copies ran while one was open for 1% -> 1% of each run, Pallas kernels for 39% -> 41%
where the time goes in v1:
time: 2020 us; the launch traced here: 2010 us
  Pallas kernels  1070 us (53%)
  waiting for transfers between devices  857 us (42%)
  starting transfers between devices  49.4 us (2%)
  local copies, waits for them, and re-layouts  21.8 us (1%)
    pallas_call x68, Pallas kernels, run(): pl.pallas_call(kern, grid_spec=pltpu.PrefetchScalarGridSpec(num_scalar_pr...  1070 us
    ppermute x19, waiting for transfers between devices, swap_y(): return lax.ppermute(v, 'replica', [(0, 1), (1, 0)])  470 us
    ppermute x16, waiting for transfers between devices, device_grads(): moved[key] = lax.ppermute(out, 'fsdp', SWAP_X)  229 us
    ppermute x8, waiting for transfers between devices, device_grads(): far_x.append(lax.ppermute(src, 'fsdp', SWAP_X))  116 us
    ppermute x9, waiting for transfers between devices, to_class(): lax.ppermute(v, ('replica', 'fsdp'), [(i, i ^ step) for i in range(8)])  42.4 us
  transfers between devices with their start and end apart: 78, of which 33 were waited for; matrix products, arithmetic and copies ran while one was open for 1% of the time, Pallas kernels for 41%

profile of v1, /device:TPU:0, one launch (start us, length us, event | category | flops | bytes accessed | tf_op | source)
XLA Modules:
  0.0 2008.2 jit_solution(9031094146403709199)
XLA Ops:
  32.6 20.4 %collective-permute-done.23.refs_3_.refs_7_ = bf16[128,4096]{1,0:T(8,128)(2,1)} collective-permute-done((bf16[128,4096]{1,0:T(8,128)(2,1)}, bf16[128,4096]{1,0:T(8,128)(2,1)}, u32[]{:S(2)}, u32[]{:S(2)}) %collective-permute-start.23) | collective-permute-done | bytes 1048608 | tf_op jit(solution)/shard_map/ppermute | solution.py:655
  56.2 19.2 collective-permute-done.17.refs_3_.refs_7_
  86.3 21.3 %collective-permute-done.5.refs_3_ = bf16[2,256,1024]{2,1,0:T(8,128)(2,1)S(1)} collective-permute-done((bf16[2,256,1024]{2,1,0:T(8,128)(2,1)}, bf16[2,256,1024]{2,1,0:T(8,128)(2,1)S(1)}, u32[]{:S(2)}, u32[]{:S(2)}) %collective-permute-start.5) | collective-permute-done | bytes 1048608 | tf_op jit(solution)/shard_map/ppermute | solution.py:672
  111.7 11.3 collective-permute-done.10.refs_3_
  147.4 12.4 collective-permute-done.8.refs_3_
  160.1 21.4 %collective-permute-done.14.refs_5_.refs_7_ = bf16[512,1024]{1,0:T(8,128)(2,1)} collective-permute-done((bf16[512,1024]{1,0:T(8,128)(2,1)}, bf16[512,1024]{1,0:T(8,128)(2,1)}, u32[]{:S(2)}, u32[]{:S(2)}) %collective-permute-start.14) | collective-permute-done | bytes 1048608 | tf_op jit(solution)/shard_map/ppermute | solution.py:643
  183.1 43.7 %shard_map.71 = (bf16[4096,4096]{1,0:T(8,128)(2,1)}, bf16[4096,4096]{1,0:T(8,128)(2,1)}, f32[8,128]{1,0:T(8,128)}) custom-call(s32[16]{0:T(128)} %stack.29.meta, bf16[4096,1024]{1,0:T(8,128)(2,1)} %get-tuple-element.165.refs_0_.refs_2_.refs_3_, bf16[4,256,4096]{2,1,0:T(8,128)(2,1)} %refs_5_.5, bf16[4,256,4096]{2,1,0:T(8,128)(2,1)} %collective-permute-done.9.refs_2_.refs_6_, ...), custom_call_target="tpu_custom_call" | custom-call | flops 30064771072 | bytes 66060288 | tf_op jit(solution)/shard_map/pallas_call | solution.py:80
  228.8 33.9 %shard_map.72 = (bf16[4096,1024]{1,0:T(8,128)(2,1)}, f32[8,128]{1,0:T(8,128)}) custom-call(s32[16]{0:T(128)} %stack.29.meta, bf16[4096,1024]{1,0:T(8,128)(2,1)} %get-tuple-element.165.refs_0_.refs_2_.refs_3_, bf16[4096,4096]{1,0:T(8,128)(2,1)} %get-tuple-element.170.refs_1_.refs_3_.refs_4_.refs_0_, bf16[4,1024,1024]{2,1,0:T(8,128)(2,1)} %refs_4_.15, ...), custom_call_target="tpu_custom_call" | custom-call | flops 30064771072 | bytes 44040192 | tf_op jit(solution)/shard_map/pallas_call | solution.py:80
  262.8 12.9 collective-permute-done.27.refs_9_.refs_6_
  276.2 62.2 %shard_map.73 = (bf16[4096,4096]{1,0:T(8,128)(2,1)}, bf16[4096,4096]{1,0:T(8,128)(2,1)}, bf16[4096,1024]{1,0:T(8,128)(2,1)}, f32[8,128]{1,0:T(8,128)}) custom-call(s32[16]{0:T(128)} %stack.29.meta, bf16[4096,1024]{1,0:T(8,128)(2,1)} %get-tuple-element.172.refs_0_.refs_2_.refs_3_, bf16[4,256,4096]{2,1,0:T(8,128)(2,1)} %refs_5_.5, ...), custom_call_target="tpu_custom_call" | custom-call | flops 60129542144 | bytes 73400320 | tf_op jit(solution)/shard_map/pallas_call | solution.py:80
  345.9 62.2 %shard_map.75 = (bf16[4096,4096]{1,0:T(8,128)(2,1)}, bf16[4096,4096]{1,0:T(8,128)(2,1)}, bf16[4096,1024]{1,0:T(8,128)(2,1)}, f32[8,128]{1,0:T(8,128)}) custom-call(s32[16]{0:T(128)} %stack.29.meta, bf16[4096,1024]{1,0:T(8,128)(2,1)} %get-tuple-element.176.refs_0_.refs_2_.refs_3_, bf16[4,256,4096]{2,1,0:T(8,128)(2,1)} %refs_5_.5, ...), custom_call_target="tpu_custom_call" | custom-call | flops 60129542144 | bytes 73400320 | tf_op jit(solution)/shard_map/pallas_call | solution.py:80
  408.2 60.5 %shard_map.76 = (bf16[4096,4096]{1,0:T(8,128)(2,1)}, bf16[4096,4096]{1,0:T(8,128)(2,1)}, f32[2,512,1024]{2,1,0:T(8,128)}, f32[2,512,1024]{2,1,0:T(8,128)}, f32[8,128]{1,0:T(8,128)}) custom-call(s32[16]{0:T(128)} %stack.29.meta, bf16[4096,1024]{1,0:T(8,128)(2,1)} %get-tuple-element.178.refs_0_.refs_2_.refs_3_, bf16[4,256,4096]{2,1,0:T(8,128)(2,1)} %refs_5_.5, ...), custom_call_target="tpu_custom_call" | custom-call | flops 45097156608 | bytes 66060288 | tf_op jit(solution)/shard_map/pallas_call | solution.py:80
  469.1 47.9 %collective-permute-done.31.refs_6_ = bf16[1024,1024]{1,0:T(8,128)(2,1)} collective-permute-done((bf16[1024,1024]{1,0:T(8,128)(2,1)}, bf16[1024,1024]{1,0:T(8,128)(2,1)}, u32[]{:S(2)}, u32[]{:S(2)}) %collective-permute-start.31) | collective-permute-done | bytes 2097184 | tf_op jit(solution)/shard_map/ppermute | solution.py:655
  525.6 37.0 %shard_map.78 = (bf16[4096,2048]{1,0:T(8,128)(2,1)}, f32[2,256,2048]{2,1,0:T(8,128)}, f32[8,128]{1,0:T(8,128)}) custom-call(s32[16]{0:T(128)} %stack.29.meta, bf16[4096,1024]{1,0:T(8,128)(2,1)} %get-tuple-element.175.refs_5_.refs_1_.refs_0_, bf16[4096,4096]{1,0:T(8,128)(2,1)} %get-tuple-element.180.refs_1_, ...), custom_call_target="tpu_custom_call" | custom-call | flops 22548578304 | bytes 36700160 | tf_op jit(solution)/shard_map/pallas_call | solution.py:80
  570.5 37.1 %shard_map.80 = (bf16[4096,2048]{1,0:T(8,128)(2,1)}, f32[2,256,2048]{2,1,0:T(8,128)}, f32[8,128]{1,0:T(8,128)}) custom-call(s32[16]{0:T(128)} %stack.29.meta, bf16[4096,1024]{1,0:T(8,128)(2,1)} %get-tuple-element.175.refs_5_.refs_1_.refs_0_, bf16[4096,4096]{1,0:T(8,128)(2,1)} %get-tuple-element.180.refs_1_, ...), custom_call_target="tpu_custom_call" | custom-call | flops 22548578304 | bytes 36700160 | tf_op jit(solution)/shard_map/pallas_call | solution.py:80
  625.4 30.6 %collective-permute-done.35.refs_3_ = f32[512,1024]{1,0:T(8,128)} collective-permute-done((f32[512,1024]{1,0:T(8,128)}, f32[512,1024]{1,0:T(8,128)}, u32[]{:S(2)}, u32[]{:S(2)}) %collective-permute-start.35) | collective-permute-done | bytes 2097184 | tf_op jit(solution)/shard_map/ppermute | solution.py:749
  664.5 50.9 %shard_map.84 = (bf16[4096,1024]{1,0:T(8,128)(2,1)}, f32[2,1024,1024]{2,1,0:T(8,128)}, f32[8,128]{1,0:T(8,128)}) custom-call(s32[16]{0:T(128)} %stack.29.meta, bf16[4096,1024]{1,0:T(8,128)(2,1)} %get-tuple-element.175.refs_5_.refs_1_.refs_0_, bf16[4096,2048]{1,0:T(8,128)(2,1)} %get-tuple-element.185.refs_1_, ...), custom_call_target="tpu_custom_call" | custom-call | flops 45097156608 | bytes 44040192 | tf_op jit(solution)/shard_map/pallas_call | solution.py:80
  717.6 46.8 %collective-permute-done.41.refs_3_ = f32[512,1024]{1,0:T(8,128)} collective-permute-done((f32[512,1024]{1,0:T(8,128)}, f32[512,1024]{1,0:T(8,128)}, u32[]{:S(2)}, u32[]{:S(2)}) %collective-permute-start.41) | collective-permute-done | bytes 2097184 | tf_op jit(solution)/shard_map/ppermute | solution.py:749
  772.7 36.6 %collective-permute-done.40.refs_3_ = f32[256,2048]{1,0:T(8,128)} collective-permute-done((f32[256,2048]{1,0:T(8,128)}, f32[256,2048]{1,0:T(8,128)}, u32[]{:S(2)}, u32[]{:S(2)}) %collective-permute-start.40) | collective-permute-done | bytes 2097184 | tf_op jit(solution)/shard_map/ppermute | solution.py:749
  809.3 9.6 shard_map.86
  819.0 11.3 shard_map.87
  830.3 23.9 %collective-permute-done.38.refs_3_ = f32[256,2048]{1,0:T(8,128)} collective-permute-done((f32[256,2048]{1,0:T(8,128)}, f32[256,2048]{1,0:T(8,128)}, u32[]{:S(2)}, u32[]{:S(2)}) %collective-permute-start.38) | collective-permute-done | bytes 2097184 | tf_op jit(solution)/shard_map/ppermute | solution.py:749
  863.5 37.0 %shard_map.89 = (bf16[4096,2048]{1,0:T(8,128)(2,1)}, f32[2,256,2048]{2,1,0:T(8,128)}, f32[8,128]{1,0:T(8,128)}) custom-call(s32[16]{0:T(128)} %stack.29.meta, bf16[4096,1024]{1,0:T(8,128)(2,1)} %get-tuple-element.198.refs_1_.refs_0_, bf16[4096,4096]{1,0:T(8,128)(2,1)} %get-tuple-element.199.refs_1_, ...), custom_call_target="tpu_custom_call" | custom-call | flops 22548578304 | bytes 36700160 | tf_op jit(solution)/shard_map/pallas_call | solution.py:80
  900.6 37.2 %shard_map.90 = (bf16[4096,2048]{1,0:T(8,128)(2,1)}, f32[2,256,2048]{2,1,0:T(8,128)}, f32[8,128]{1,0:T(8,128)}) custom-call(s32[16]{0:T(128)} %stack.29.meta, bf16[4096,1024]{1,0:T(8,128)(2,1)} %get-tuple-element.198.refs_1_.refs_0_, bf16[4096,4096]{1,0:T(8,128)(2,1)} %get-tuple-element.199.refs_1_, ...), custom_call_target="tpu_custom_call" | custom-call | flops 22548578304 | bytes 36700160 | tf_op jit(solution)/shard_map/pallas_call | solution.py:80
  946.9 11.9 shard_map.92
  967.5 50.8 %shard_map.94 = (bf16[4096,1024]{1,0:T(8,128)(2,1)}, f32[2,1024,1024]{2,1,0:T(8,128)}, f32[8,128]{1,0:T(8,128)}) custom-call(s32[16]{0:T(128)} %stack.29.meta, bf16[4096,1024]{1,0:T(8,128)(2,1)} %get-tuple-element.198.refs_1_.refs_0_, bf16[4096,2048]{1,0:T(8,128)(2,1)} %get-tuple-element.210.refs_1_, bf16[4096,2048]{1,0:T(8,128)(2,1)} %get-tuple-element.211.refs_1_.refs_2_, ...), custom_call_target="tpu_custom_call" | custom-call | flops 45097156608 | bytes 44040192 | tf_op jit(solution)/shard_map/pallas_call | solution.py:80
  1020.4 46.8 %collective-permute-done.47.refs_3_ = f32[256,2048]{1,0:T(8,128)} collective-permute-done((f32[256,2048]{1,0:T(8,128)}, f32[256,2048]{1,0:T(8,128)}, u32[]{:S(2)}, u32[]{:S(2)}) %collective-permute-start.47) | collective-permute-done | bytes 2097184 | tf_op jit(solution)/shard_map/ppermute | solution.py:749
  1067.2 9.7 shard_map.95
  1076.9 11.3 shard_map.96
  1088.2 37.0 %shard_map.97 = (bf16[4096,2048]{1,0:T(8,128)(2,1)}, f32[2,256,2048]{2,1,0:T(8,128)}, f32[8,128]{1,0:T(8,128)}) custom-call(s32[16]{0:T(128)} %stack.29.meta, bf16[4096,1024]{1,0:T(8,128)(2,1)} %get-tuple-element.220.refs_1_.refs_0_, bf16[4096,4096]{1,0:T(8,128)(2,1)} %get-tuple-element.221.refs_1_, ...), custom_call_target="tpu_custom_call" | custom-call | flops 22548578304 | bytes 36700160 | tf_op jit(solution)/shard_map/pallas_call | solution.py:80
  1134.8 37.0 %shard_map.99 = (bf16[4096,2048]{1,0:T(8,128)(2,1)}, f32[2,256,2048]{2,1,0:T(8,128)}, f32[8,128]{1,0:T(8,128)}) custom-call(s32[16]{0:T(128)} %stack.29.meta, bf16[4096,1024]{1,0:T(8,128)(2,1)} %get-tuple-element.220.refs_1_.refs_0_, bf16[4096,4096]{1,0:T(8,128)(2,1)} %get-tuple-element.221.refs_1_, ...), custom_call_target="tpu_custom_call" | custom-call | flops 22548578304 | bytes 36700160 | tf_op jit(solution)/shard_map/pallas_call | solution.py:80
  1172.3 29.2 %collective-permute-done.50.refs_3_ = f32[1024,1024]{1,0:T(8,128)} collective-permute-done((f32[1024,1024]{1,0:T(8,128)}, f32[1024,1024]{1,0:T(8,128)}, u32[]{:S(2)}, u32[]{:S(2)}) %collective-permute-start.50) | collective-permute-done | bytes 4194336 | tf_op jit(solution)/shard_map/ppermute | solution.py:749
  1201.5 11.9 shard_map.100
  1231.0 51.0 %shard_map.103 = (bf16[4096,1024]{1,0:T(8,128)(2,1)}, f32[2,1024,1024]{2,1,0:T(8,128)}, f32[8,128]{1,0:T(8,128)}) custom-call(s32[16]{0:T(128)} %stack.29.meta, bf16[4096,1024]{1,0:T(8,128)(2,1)} %get-tuple-element.220.refs_1_.refs_0_, bf16[4096,2048]{1,0:T(8,128)(2,1)} %get-tuple-element.230.refs_1_, bf16[4096,2048]{1,0:T(8,128)(2,1)} %get-tuple-element.231.refs_1_.refs_2_, ...), custom_call_target="tpu_custom_call" | custom-call | flops 45097156608 | bytes 44040192 | tf_op jit(solution)/shard_map/pallas_call | solution.py:80
  1286.0 44.8 %collective-permute-done.53.refs_1_ = f32[256,2048]{1,0:T(8,128)} collective-permute-done((f32[256,2048]{1,0:T(8,128)}, f32[256,2048]{1,0:T(8,128)}, u32[]{:S(2)}, u32[]{:S(2)}) %collective-permute-start.53) | collective-permute-done | bytes 2097184 | tf_op jit(solution)/shard_map/ppermute | solution.py:643
  1362.8 13.1 collective-permute-done.55.refs_3_
  1385.5 36.8 %shard_map.109 = (bf16[4096,2048]{1,0:T(8,128)(2,1)}, f32[2,256,2048]{2,1,0:T(8,128)}, f32[8,128]{1,0:T(8,128)}) custom-call(s32[16]{0:T(128)} %stack.29.meta, bf16[4096,1024]{1,0:T(8,128)(2,1)} %get-tuple-element.239.refs_1_.refs_0_, bf16[4096,4096]{1,0:T(8,128)(2,1)} %get-tuple-element.240.refs_1_, ...), custom_call_target="tpu_custom_call" | custom-call | flops 22548578304 | bytes 36700160 | tf_op jit(solution)/shard_map/pallas_call | solution.py:80
  1432.6 36.8 %shard_map.111 = (bf16[4096,2048]{1,0:T(8,128)(2,1)}, f32[2,256,2048]{2,1,0:T(8,128)}, f32[8,128]{1,0:T(8,128)}) custom-call(s32[16]{0:T(128)} %stack.29.meta, bf16[4096,1024]{1,0:T(8,128)(2,1)} %get-tuple-element.239.refs_1_.refs_0_, bf16[4096,4096]{1,0:T(8,128)(2,1)} %get-tuple-element.240.refs_1_, ...), custom_call_target="tpu_custom_call" | custom-call | flops 22548578304 | bytes 36700160 | tf_op jit(solution)/shard_map/pallas_call | solution.py:80
  1469.9 40.6 %collective-permute-done.66.refs_1_ = f32[1024,1024]{1,0:T(8,128)} collective-permute-done((f32[1024,1024]{1,0:T(8,128)}, f32[1024,1024]{1,0:T(8,128)}, u32[]{:S(2)}, u32[]{:S(2)}) %collective-permute-start.66) | collective-permute-done | bytes 4194336 | tf_op jit(solution)/shard_map/ppermute | solution.py:643
  1510.6 44.9 %collective-permute-done.61.refs_1_ = f32[256,2048]{1,0:T(8,128)} collective-permute-done((f32[256,2048]{1,0:T(8,128)}, f32[256,2048]{1,0:T(8,128)}, u32[]{:S(2)}, u32[]{:S(2)}) %collective-permute-start.61) | collective-permute-done | bytes 2097184 | tf_op jit(solution)/shard_map/ppermute | solution.py:643
  1574.2 71.2 %collective-permute-done.60.refs_1_ = f32[1024,1024]{1,0:T(8,128)} collective-permute-done((f32[1024,1024]{1,0:T(8,128)}, f32[1024,1024]{1,0:T(8,128)}, u32[]{:S(2)}, u32[]{:S(2)}) %collective-permute-start.60) | collective-permute-done | bytes 4194336 | tf_op jit(solution)/shard_map/ppermute | solution.py:643
  1645.4 44.9 %collective-permute-done.69.refs_1_ = f32[256,2048]{1,0:T(8,128)} collective-permute-done((f32[256,2048]{1,0:T(8,128)}, f32[256,2048]{1,0:T(8,128)}, u32[]{:S(2)}, u32[]{:S(2)}) %collective-permute-start.69) | collective-permute-done | bytes 2097184 | tf_op jit(solution)/shard_map/ppermute | solution.py:643
  1702.6 32.7 %collective-permute-done.68.refs_1_ = f32[256,2048]{1,0:T(8,128)} collective-permute-done((f32[256,2048]{1,0:T(8,128)}, f32[256,2048]{1,0:T(8,128)}, u32[]{:S(2)}, u32[]{:S(2)}) %collective-permute-start.68) | collective-permute-done | bytes 2097184 | tf_op jit(solution)/shard_map/ppermute | solution.py:643
  1766.5 13.8 collective-permute-done.67.refs_1_
  1830.1 40.1 %collective-permute-done.64.refs_1_ = f32[512,1024]{1,0:T(8,128)} collective-permute-done((f32[512,1024]{1,0:T(8,128)}, f32[512,1024]{1,0:T(8,128)}, u32[]{:S(2)}, u32[]{:S(2)}) %collective-permute-start.64) | collective-permute-done | bytes 2097184 | tf_op jit(solution)/shard_map/ppermute | solution.py:643
  1882.7 54.8 %collective-permute-done.76.refs_1_ = f32[256,1024]{1,0:T(8,128)} collective-permute-done((f32[256,1024]{1,0:T(8,128)}, f32[256,1024]{1,0:T(8,128)}, u32[]{:S(2)}, u32[]{:S(2)}) %collective-permute-start.76) | collective-permute-done | bytes 1048608 | tf_op jit(solution)/shard_map/ppermute | solution.py:643
  1940.8 41.7 %collective-permute-done.75.refs_1_ = f32[256,1024]{1,0:T(8,128)} collective-permute-done((f32[256,1024]{1,0:T(8,128)}, f32[256,1024]{1,0:T(8,128)}, u32[]{:S(2)}, u32[]{:S(2)}) %collective-permute-start.75) | collective-permute-done | bytes 1048608 | tf_op jit(solution)/shard_map/ppermute | solution.py:643
  1993.0 11.5 collective-permute-done.73.refs_1_
  (206 shorter events, 389.2 us)
Async XLA Ops:
  0.6 182.3 %collective-permute-start.9 = (bf16[4,256,4096]{2,1,0:T(8,128)(2,1)}, bf16[4,256,4096]{2,1,0:T(8,128)(2,1)}, u32[]{:S(2)}, u32[]{:S(2)}) collective-permute-start(bf16[4,256,4096]{2,1,0:T(8,128)(2,1)} %refs_5_.5), channel_id=1, source_target_pairs={{0,1},{1,0},{2,3},{3,2},{4,5},{5,4},{6,7},{7,6}} | collective-permute-start | bytes 25165832 | tf_op jit(solution)/shard_map/ppermute | solution.py:640
  17.5 210.8 %collective-permute-start.12 = (bf16[4,1024,1024]{2,1,0:T(8,128)(2,1)}, bf16[4,1024,1024]{2,1,0:T(8,128)(2,1)}, u32[]{:S(2)}, u32[]{:S(2)}) collective-permute-start(bf16[4,1024,1024]{2,1,0:T(8,128)(2,1)} %refs_4_.15), channel_id=1, source_target_pairs={{0,1},{1,0},{2,3},{3,2},{4,5},{5,4},{6,7},{7,6}} | collective-permute-start | bytes 25165832 | tf_op jit(solution)/shard_map/ppermute | solution.py:640
  19.6 55.8 %collective-permute-start.17 = (bf16[128,4096]{1,0:T(8,128)(2,1)}, bf16[128,4096]{1,0:T(8,128)(2,1)}, u32[]{:S(2)}, u32[]{:S(2)}) collective-permute-start(bf16[128,4096]{1,0:T(8,128)(2,1)} %get-tuple-element.322), channel_id=1, source_target_pairs={{0,2},{2,0},{1,3},{3,1},{4,6},{6,4},{5,7},{7,5}} | collective-permute-start | bytes 3145736 | tf_op jit(solution)/shard_map/ppermute | solution.py:655
  30.6 51.5 %collective-permute-start.4 = (bf16[2,256,1024]{2,1,0:T(8,128)(2,1)}, bf16[2,256,1024]{2,1,0:T(8,128)(2,1)}, u32[]{:S(2)}, u32[]{:S(2)}) collective-permute-start(bf16[2,256,1024]{2,1,0:T(8,128)(2,1)} %get-tuple-element.161), channel_id=1, source_target_pairs={{0,4},{1,5},{2,6},{3,7},{4,0},{5,1},{6,2},{7,3}} | collective-permute-start | bytes 3145736 | tf_op jit(solution)/shard_map/ppermute | solution.py:672
  53.1 81.0 %collective-permute-start.3 = (bf16[2,768,1024]{2,1,0:T(8,128)(2,1)}, bf16[2,768,1024]{2,1,0:T(8,128)(2,1)}, u32[]{:S(2)}, u32[]{:S(2)}) collective-permute-start(bf16[2,768,1024]{2,1,0:T(8,128)(2,1)} %get-tuple-element.160), channel_id=1, source_target_pairs={{0,1},{1,0},{2,3},{3,2},{4,5},{5,4},{6,7},{7,6}} | collective-permute-start | bytes 9437192 | tf_op jit(solution)/shard_map/ppermute | solution.py:672
  123.1 58.9 %collective-permute-start.11 = (bf16[256,4096]{1,0:T(8,128)(2,1)}, bf16[256,4096]{1,0:T(8,128)(2,1)}, u32[]{:S(2)}, u32[]{:S(2)}) collective-permute-start(bf16[256,4096]{1,0:T(8,128)(2,1)} %collective-permute-done.10.refs_3_), channel_id=1, source_target_pairs={{0,1},{1,0},{2,3},{3,2},{4,5},{5,4},{6,7},{7,6}} | collective-permute-start | bytes 6291464 | tf_op jit(solution)/shard_map/ppermute | solution.py:640
  159.8 67.5 %collective-permute-start.21 = (bf16[1024,1024]{1,0:T(8,128)(2,1)}, bf16[1024,1024]{1,0:T(8,128)(2,1)}, u32[]{:S(2)}, u32[]{:S(2)}) collective-permute-start(bf16[1024,1024]{1,0:T(8,128)(2,1)} %get-tuple-element.320), channel_id=1, source_target_pairs={{0,2},{2,0},{1,3},{3,1},{4,6},{6,4},{5,7},{7,5}} | collective-permute-start | bytes 6291464 | tf_op jit(solution)/shard_map/ppermute | solution.py:655
  226.8 48.8 %collective-permute-start.27 = (bf16[1024,1024]{1,0:T(8,128)(2,1)}, bf16[1024,1024]{1,0:T(8,128)(2,1)}, u32[]{:S(2)}, u32[]{:S(2)}) collective-permute-start(bf16[1024,1024]{1,0:T(8,128)(2,1)} %get-tuple-element.319), channel_id=1, source_target_pairs={{0,2},{2,0},{1,3},{3,1},{4,6},{6,4},{5,7},{7,5}} | collective-permute-start | bytes 6291464 | tf_op jit(solution)/shard_map/ppermute | solution.py:655
  262.7 75.7 %collective-permute-start.29 = (bf16[256,4096]{1,0:T(8,128)(2,1)}, bf16[256,4096]{1,0:T(8,128)(2,1)}, u32[]{:S(2)}, u32[]{:S(2)}) collective-permute-start(bf16[256,4096]{1,0:T(8,128)(2,1)} %slice_bitcast_fusion.1), channel_id=1, source_target_pairs={{0,2},{2,0},{1,3},{3,1},{4,6},{6,4},{5,7},{7,5}} | collective-permute-start | bytes 6291464 | tf_op jit(solution)/shard_map/ppermute | solution.py:655
  262.8 76.1 %collective-permute-start.6 = (bf16[2,768,1024]{2,1,0:T(8,128)(2,1)}, bf16[2,768,1024]{2,1,0:T(8,128)(2,1)}, u32[]{:S(2)}, u32[]{:S(2)}) collective-permute-start(bf16[2,768,1024]{2,1,0:T(8,128)(2,1)} %get-tuple-element.166), channel_id=1, source_target_pairs={{0,1},{1,0},{2,3},{3,2},{4,5},{5,4},{6,7},{7,6}} | collective-permute-start | bytes 9437192 | tf_op jit(solution)/shard_map/ppermute | solution.py:672
  275.7 70.2 %collective-permute-start.25 = (bf16[128,4096]{1,0:T(8,128)(2,1)}, bf16[128,4096]{1,0:T(8,128)(2,1)}, u32[]{:S(2)}, u32[]{:S(2)}) collective-permute-start(bf16[128,4096]{1,0:T(8,128)(2,1)} %collective-permute-done.23.refs_3_.refs_7_), channel_id=1, source_target_pairs={{0,1},{1,0},{2,3},{3,2},{4,5},{5,4},{6,7},{7,6}} | collective-permute-start | bytes 3145736 | tf_op jit(solution)/shard_map/ppermute | solution.py:640
  275.7 70.2 %collective-permute-start.26 = (bf16[128,4096]{1,0:T(8,128)(2,1)}, bf16[128,4096]{1,0:T(8,128)(2,1)}, u32[]{:S(2)}, u32[]{:S(2)}) collective-permute-start(bf16[128,4096]{1,0:T(8,128)(2,1)} %collective-permute-done.24.refs_4_.refs_8_), channel_id=1, source_target_pairs={{0,1},{1,0},{2,3},{3,2},{4,5},{5,4},{6,7},{7,6}} | collective-permute-start | bytes 3145736 | tf_op jit(solution)/shard_map/ppermute | solution.py:640
  276.2 69.7 %collective-permute-start.28 = (bf16[1024,1024]{1,0:T(8,128)(2,1)}, bf16[1024,1024]{1,0:T(8,128)(2,1)}, u32[]{:S(2)}, u32[]{:S(2)}) collective-permute-start(bf16[1024,1024]{1,0:T(8,128)(2,1)} %collective-permute-done.27.refs_9_.refs_6_), channel_id=1, source_target_pairs={{0,1},{1,0},{2,3},{3,2},{4,5},{5,4},{6,7},{7,6}} | collective-permute-start | bytes 6291464 | tf_op jit(solution)/shard_map/ppermute | solution.py:640
  338.4 69.8 %collective-permute-start.30 = (bf16[256,4096]{1,0:T(8,128)(2,1)}, bf16[256,4096]{1,0:T(8,128)(2,1)}, u32[]{:S(2)}, u32[]{:S(2)}) collective-permute-start(bf16[256,4096]{1,0:T(8,128)(2,1)} %collective-permute-done.29.refs_3_.refs_7_), channel_id=1, source_target_pairs={{0,1},{1,0},{2,3},{3,2},{4,5},{5,4},{6,7},{7,6}} | collective-permute-start | bytes 6291464 | tf_op jit(solution)/shard_map/ppermute | solution.py:640
  468.7 48.9 %collective-permute-start.33 = (f32[2,512,1024]{2,1,0:T(8,128)}, f32[2,512,1024]{2,1,0:T(8,128)}, u32[]{:S(2)}, u32[]{:S(2)}) collective-permute-start(f32[2,512,1024]{2,1,0:T(8,128)} %get-tuple-element.182), channel_id=1, source_target_pairs={{0,1},{1,0},{2,3},{3,2},{4,5},{5,4},{6,7},{7,6}} | collective-permute-start | bytes 12582920 | tf_op jit(solution)/shard_map/ppermute | solution.py:640
  715.5 103.5 %collective-permute-start.39 = (f32[2,1024,1024]{2,1,0:T(8,128)}, f32[2,1024,1024]{2,1,0:T(8,128)}, u32[]{:S(2)}, u32[]{:S(2)}) collective-permute-start(f32[2,1024,1024]{2,1,0:T(8,128)} %get-tuple-element.201), channel_id=1, source_target_pairs={{0,1},{1,0},{2,3},{3,2},{4,5},{5,4},{6,7},{7,6}} | collective-permute-start | bytes 25165832 | tf_op jit(solution)/shard_map/ppermute | solution.py:640
  715.6 93.7 %collective-permute-start.40 = (f32[256,2048]{1,0:T(8,128)}, f32[256,2048]{1,0:T(8,128)}, u32[]{:S(2)}, u32[]{:S(2)}) collective-permute-start(f32[256,2048]{1,0:T(8,128)} %get-tuple-element.202), channel_id=1, source_target_pairs={{0,2},{2,0},{1,3},{3,1},{4,6},{6,4},{5,7},{7,5}} | collective-permute-start | bytes 6291464 | tf_op jit(solution)/shard_map/ppermute | solution.py:749
  717.6 136.7 %collective-permute-start.38 = (f32[256,2048]{1,0:T(8,128)}, f32[256,2048]{1,0:T(8,128)}, u32[]{:S(2)}, u32[]{:S(2)}) collective-permute-start(f32[256,2048]{1,0:T(8,128)} %get-tuple-element.200), channel_id=1, source_target_pairs={{0,2},{2,0},{1,3},{3,1},{4,6},{6,4},{5,7},{7,5}} | collective-permute-start | bytes 6291464 | tf_op jit(solution)/shard_map/ppermute | solution.py:749
  830.3 116.6 %collective-permute-start.43 = (f32[1024,1024]{1,0:T(8,128)}, f32[1024,1024]{1,0:T(8,128)}, u32[]{:S(2)}, u32[]{:S(2)}) collective-permute-start(f32[1024,1024]{1,0:T(8,128)} %get-tuple-element.214), channel_id=1, source_target_pairs={{0,2},{2,0},{1,3},{3,1},{4,6},{6,4},{5,7},{7,5}} | collective-permute-start | bytes 12582920 | tf_op jit(solution)/shard_map/ppermute | solution.py:749
  1018.3 58.6 %collective-permute-start.46 = (f32[2,1024,1024]{2,1,0:T(8,128)}, f32[2,1024,1024]{2,1,0:T(8,128)}, u32[]{:S(2)}, u32[]{:S(2)}) collective-permute-start(f32[2,1024,1024]{2,1,0:T(8,128)} %get-tuple-element.223), channel_id=1, source_target_pairs={{0,1},{1,0},{2,3},{3,2},{4,5},{5,4},{6,7},{7,6}} | collective-permute-start | bytes 25165832 | tf_op jit(solution)/shard_map/ppermute | solution.py:640
  1018.4 106.9 %collective-permute-start.45 = (f32[256,2048]{1,0:T(8,128)}, f32[256,2048]{1,0:T(8,128)}, u32[]{:S(2)}, u32[]{:S(2)}) collective-permute-start(f32[256,2048]{1,0:T(8,128)} %get-tuple-element.222), channel_id=1, source_target_pairs={{0,2},{2,0},{1,3},{3,1},{4,6},{6,4},{5,7},{7,5}} | collective-permute-start | bytes 6291464 | tf_op jit(solution)/shard_map/ppermute | solution.py:749
  1088.2 113.3 %collective-permute-start.50 = (f32[1024,1024]{1,0:T(8,128)}, f32[1024,1024]{1,0:T(8,128)}, u32[]{:S(2)}, u32[]{:S(2)}) collective-permute-start(f32[1024,1024]{1,0:T(8,128)} %get-tuple-element.234), channel_id=1, source_target_pairs={{0,2},{2,0},{1,3},{3,1},{4,6},{6,4},{5,7},{7,5}} | collective-permute-start | bytes 12582920 | tf_op jit(solution)/shard_map/ppermute | solution.py:749
  1125.3 88.1 %collective-permute-start.49 = (f32[2,256,2048]{2,1,0:T(8,128)}, f32[2,256,2048]{2,1,0:T(8,128)}, u32[]{:S(2)}, u32[]{:S(2)}) collective-permute-start(f32[2,256,2048]{2,1,0:T(8,128)} %get-tuple-element.233), channel_id=1, source_target_pairs={{0,1},{1,0},{2,3},{3,2},{4,5},{5,4},{6,7},{7,6}} | collective-permute-start | bytes 12582920 | tf_op jit(solution)/shard_map/ppermute | solution.py:640
  1171.8 50.6 %collective-permute-start.48 = (f32[2,256,2048]{2,1,0:T(8,128)}, f32[2,256,2048]{2,1,0:T(8,128)}, u32[]{:S(2)}, u32[]{:S(2)}) collective-permute-start(f32[2,256,2048]{2,1,0:T(8,128)} %get-tuple-element.232), channel_id=1, source_target_pairs={{0,1},{1,0},{2,3},{3,2},{4,5},{5,4},{6,7},{7,6}} | collective-permute-start | bytes 12582920 | tf_op jit(solution)/shard_map/ppermute | solution.py:640
  1281.9 64.1 %collective-permute-start.51 = (f32[2,1024,1024]{2,1,0:T(8,128)}, f32[2,1024,1024]{2,1,0:T(8,128)}, u32[]{:S(2)}, u32[]{:S(2)}) collective-permute-start(f32[2,1024,1024]{2,1,0:T(8,128)} %get-tuple-element.241), channel_id=1, source_target_pairs={{0,1},{1,0},{2,3},{3,2},{4,5},{5,4},{6,7},{7,6}} | collective-permute-start | bytes 25165832 | tf_op jit(solution)/shard_map/ppermute | solution.py:640
  1282.0 48.8 %collective-permute-start.53 = (f32[256,2048]{1,0:T(8,128)}, f32[256,2048]{1,0:T(8,128)}, u32[]{:S(2)}, u32[]{:S(2)}) collective-permute-start(f32[256,2048]{1,0:T(8,128)} %get-tuple-element.243.refs_0_), channel_id=1, source_target_pairs={{0,4},{4,0},{1,5},{5,1},{2,6},{6,2},{3,7},{7,3}} | collective-permute-start | bytes 6291464 | tf_op jit(solution)/shard_map/ppermute | solution.py:643
  1283.0 52.8 %collective-permute-start.52 = (f32[256,2048]{1,0:T(8,128)}, f32[256,2048]{1,0:T(8,128)}, u32[]{:S(2)}, u32[]{:S(2)}) collective-permute-start(f32[256,2048]{1,0:T(8,128)} %get-tuple-element.242), channel_id=1, source_target_pairs={{0,2},{2,0},{1,3},{3,1},{4,6},{6,4},{5,7},{7,5}} | collective-permute-start | bytes 6291464 | tf_op jit(solution)/shard_map/ppermute | solution.py:749
  1283.0 93.0 %collective-permute-start.55 = (f32[256,2048]{1,0:T(8,128)}, f32[256,2048]{1,0:T(8,128)}, u32[]{:S(2)}, u32[]{:S(2)}) collective-permute-start(f32[256,2048]{1,0:T(8,128)} %get-tuple-element.248), channel_id=1, source_target_pairs={{0,2},{2,0},{1,3},{3,1},{4,6},{6,4},{5,7},{7,5}} | collective-permute-start | bytes 6291464 | tf_op jit(solution)/shard_map/ppermute | solution.py:749
  1285.0 147.6 %collective-permute-start.70 = (f32[256,2048]{1,0:T(8,128)}, f32[256,2048]{1,0:T(8,128)}, u32[]{:S(2)}, u32[]{:S(2)}) collective-permute-start(f32[256,2048]{1,0:T(8,128)} %get-tuple-element.282.refs_0_), channel_id=1, source_target_pairs={{0,4},{4,0},{1,5},{5,1},{2,6},{6,2},{3,7},{7,3}} | collective-permute-start | bytes 6291464 | tf_op jit(solution)/shard_map/ppermute | solution.py:643
  1330.8 138.6 %collective-permute-start.62 = (f32[256,2048]{1,0:T(8,128)}, f32[256,2048]{1,0:T(8,128)}, u32[]{:S(2)}, u32[]{:S(2)}) collective-permute-start(f32[256,2048]{1,0:T(8,128)} %get-tuple-element.264.refs_0_), channel_id=1, source_target_pairs={{0,4},{4,0},{1,5},{5,1},{2,6},{6,2},{3,7},{7,3}} | collective-permute-start | bytes 6291464 | tf_op jit(solution)/shard_map/ppermute | solution.py:643
  1335.7 174.9 %collective-permute-start.66 = (f32[1024,1024]{1,0:T(8,128)}, f32[1024,1024]{1,0:T(8,128)}, u32[]{:S(2)}, u32[]{:S(2)}) collective-permute-start(f32[1024,1024]{1,0:T(8,128)} %get-tuple-element.277.refs_0_), channel_id=1, source_target_pairs={{0,4},{4,0},{1,5},{5,1},{2,6},{6,2},{3,7},{7,3}} | collective-permute-start | bytes 12582920 | tf_op jit(solution)/shard_map/ppermute | solution.py:643
  1346.0 209.5 %collective-permute-start.61 = (f32[256,2048]{1,0:T(8,128)}, f32[256,2048]{1,0:T(8,128)}, u32[]{:S(2)}, u32[]{:S(2)}) collective-permute-start(f32[256,2048]{1,0:T(8,128)} %get-tuple-element.263.refs_0_), channel_id=1, source_target_pairs={{0,4},{4,0},{1,5},{5,1},{2,6},{6,2},{3,7},{7,3}} | collective-permute-start | bytes 6291464 | tf_op jit(solution)/shard_map/ppermute | solution.py:643
  1423.1 222.3 %collective-permute-start.60 = (f32[1024,1024]{1,0:T(8,128)}, f32[1024,1024]{1,0:T(8,128)}, u32[]{:S(2)}, u32[]{:S(2)}) collective-permute-start(f32[1024,1024]{1,0:T(8,128)} %get-tuple-element.262.refs_0_), channel_id=1, source_target_pairs={{0,4},{4,0},{1,5},{5,1},{2,6},{6,2},{3,7},{7,3}} | collective-permute-start | bytes 12582920 | tf_op jit(solution)/shard_map/ppermute | solution.py:643
  1432.5 134.3 %collective-permute-start.57 = (f32[2,256,2048]{2,1,0:T(8,128)}, f32[2,256,2048]{2,1,0:T(8,128)}, u32[]{:S(2)}, u32[]{:S(2)}) collective-permute-start(f32[2,256,2048]{2,1,0:T(8,128)} %get-tuple-element.257), channel_id=1, source_target_pairs={{0,1},{1,0},{2,3},{3,2},{4,5},{5,4},{6,7},{7,6}} | collective-permute-start | bytes 12582920 | tf_op jit(solution)/shard_map/ppermute | solution.py:640
  1469.4 225.8 %collective-permute-start.56 = (f32[2,256,2048]{2,1,0:T(8,128)}, f32[2,256,2048]{2,1,0:T(8,128)}, u32[]{:S(2)}, u32[]{:S(2)}) collective-permute-start(f32[2,256,2048]{2,1,0:T(8,128)} %get-tuple-element.255), channel_id=1, source_target_pairs={{0,1},{1,0},{2,3},{3,2},{4,5},{5,4},{6,7},{7,6}} | collective-permute-start | bytes 12582920 | tf_op jit(solution)/shard_map/ppermute | solution.py:640
  1555.5 134.8 %collective-permute-start.69 = (f32[256,2048]{1,0:T(8,128)}, f32[256,2048]{1,0:T(8,128)}, u32[]{:S(2)}, u32[]{:S(2)}) collective-permute-start(f32[256,2048]{1,0:T(8,128)} %get-tuple-element.281.refs_0_), channel_id=1, source_target_pairs={{0,4},{4,0},{1,5},{5,1},{2,6},{6,2},{3,7},{7,3}} | collective-permute-start | bytes 6291464 | tf_op jit(solution)/shard_map/ppermute | solution.py:643
  1557.6 177.7 %collective-permute-start.68 = (f32[256,2048]{1,0:T(8,128)}, f32[256,2048]{1,0:T(8,128)}, u32[]{:S(2)}, u32[]{:S(2)}) collective-permute-start(f32[256,2048]{1,0:T(8,128)} %get-tuple-element.280.refs_0_), channel_id=1, source_target_pairs={{0,4},{4,0},{1,5},{5,1},{2,6},{6,2},{3,7},{7,3}} | collective-permute-start | bytes 6291464 | tf_op jit(solution)/shard_map/ppermute | solution.py:643
  1566.8 213.4 %collective-permute-start.67 = (f32[512,1024]{1,0:T(8,128)}, f32[512,1024]{1,0:T(8,128)}, u32[]{:S(2)}, u32[]{:S(2)}) collective-permute-start(f32[512,1024]{1,0:T(8,128)} %get-tuple-element.278.refs_0_), channel_id=1, source_target_pairs={{0,4},{4,0},{1,5},{5,1},{2,6},{6,2},{3,7},{7,3}} | collective-permute-start | bytes 6291464 | tf_op jit(solution)/shard_map/ppermute | solution.py:643
  1645.4 106.5 %collective-permute-start.59 = (f32[256,1024]{1,0:T(8,128)}, f32[256,1024]{1,0:T(8,128)}, u32[]{:S(2)}, u32[]{:S(2)}) collective-permute-start(f32[256,1024]{1,0:T(8,128)} %get-tuple-element.261), channel_id=1, source_target_pairs={{0,2},{2,0},{1,3},{3,1},{4,6},{6,4},{5,7},{7,5}} | collective-permute-start | bytes 3145736 | tf_op jit(solution)/shard_map/ppermute | solution.py:749
  1690.3 134.8 %collective-permute-start.65 = (f32[512,1024]{1,0:T(8,128)}, f32[512,1024]{1,0:T(8,128)}, u32[]{:S(2)}, u32[]{:S(2)}) collective-permute-start(f32[512,1024]{1,0:T(8,128)} %get-tuple-element.276.refs_0_), channel_id=1, source_target_pairs={{0,4},{4,0},{1,5},{5,1},{2,6},{6,2},{3,7},{7,3}} | collective-permute-start | bytes 6291464 | tf_op jit(solution)/shard_map/ppermute | solution.py:643
  1695.2 174.9 %collective-permute-start.64 = (f32[512,1024]{1,0:T(8,128)}, f32[512,1024]{1,0:T(8,128)}, u32[]{:S(2)}, u32[]{:S(2)}) collective-permute-start(f32[512,1024]{1,0:T(8,128)} %get-tuple-element.275.refs_0_), channel_id=1, source_target_pairs={{0,4},{4,0},{1,5},{5,1},{2,6},{6,2},{3,7},{7,3}} | collective-permute-start | bytes 6291464 | tf_op jit(solution)/shard_map/ppermute | solution.py:643
  1751.9 58.0 %collective-permute-start.72 = (f32[256,1024]{1,0:T(8,128)}, f32[256,1024]{1,0:T(8,128)}, u32[]{:S(2)}, u32[]{:S(2)}) collective-permute-start(f32[256,1024]{1,0:T(8,128)} %get-tuple-element.295), channel_id=1, source_target_pairs={{0,2},{2,0},{1,3},{3,1},{4,6},{6,4},{5,7},{7,5}} | collective-permute-start | bytes 3145736 | tf_op jit(solution)/shard_map/ppermute | solution.py:749
  1780.2 94.8 %collective-permute-start.63 = (f32[256,1024]{1,0:T(8,128)}, f32[256,1024]{1,0:T(8,128)}, u32[]{:S(2)}, u32[]{:S(2)}) collective-permute-start(f32[256,1024]{1,0:T(8,128)} %get-tuple-element.274), channel_id=1, source_target_pairs={{0,2},{2,0},{1,3},{3,1},{4,6},{6,4},{5,7},{7,5}} | collective-permute-start | bytes 3145736 | tf_op jit(solution)/shard_map/ppermute | solution.py:749
  1780.2 208.8 %collective-permute-start.77 = (f32[512,1024]{1,0:T(8,128)}, f32[512,1024]{1,0:T(8,128)}, u32[]{:S(2)}, u32[]{:S(2)}) collective-permute-start(f32[512,1024]{1,0:T(8,128)} %get-tuple-element.312.refs_0_), channel_id=1, source_target_pairs={{0,4},{4,0},{1,5},{5,1},{2,6},{6,2},{3,7},{7,3}} | collective-permute-start | bytes 6291464 | tf_op jit(solution)/shard_map/ppermute | solution.py:643
  1809.9 127.6 %collective-permute-start.76 = (f32[256,1024]{1,0:T(8,128)}, f32[256,1024]{1,0:T(8,128)}, u32[]{:S(2)}, u32[]{:S(2)}) collective-permute-start(f32[256,1024]{1,0:T(8,128)} %get-tuple-element.304.refs_0_), channel_id=1, source_target_pairs={{0,4},{4,0},{1,5},{5,1},{2,6},{6,2},{3,7},{7,3}} | collective-permute-start | bytes 3145736 | tf_op jit(solution)/shard_map/ppermute | solution.py:643
  1825.2 160.6 %collective-permute-start.74 = (f32[256,1024]{1,0:T(8,128)}, f32[256,1024]{1,0:T(8,128)}, u32[]{:S(2)}, u32[]{:S(2)}) collective-permute-start(f32[256,1024]{1,0:T(8,128)} %get-tuple-element.302.refs_0_), channel_id=1, source_target_pairs={{0,4},{4,0},{1,5},{5,1},{2,6},{6,2},{3,7},{7,3}} | collective-permute-start | bytes 3145736 | tf_op jit(solution)/shard_map/ppermute | solution.py:643
  1870.1 112.4 %collective-permute-start.75 = (f32[256,1024]{1,0:T(8,128)}, f32[256,1024]{1,0:T(8,128)}, u32[]{:S(2)}, u32[]{:S(2)}) collective-permute-start(f32[256,1024]{1,0:T(8,128)} %get-tuple-element.303.refs_0_), channel_id=1, source_target_pairs={{0,4},{4,0},{1,5},{5,1},{2,6},{6,2},{3,7},{7,3}} | collective-permute-start | bytes 3145736 | tf_op jit(solution)/shard_map/ppermute | solution.py:643
  1881.6 122.8 %collective-permute-start.73 = (f32[256,1024]{1,0:T(8,128)}, f32[256,1024]{1,0:T(8,128)}, u32[]{:S(2)}, u32[]{:S(2)}) collective-permute-start(f32[256,1024]{1,0:T(8,128)} %get-tuple-element.301.refs_0_), channel_id=1, source_target_pairs={{0,4},{4,0},{1,5},{5,1},{2,6},{6,2},{3,7},{7,3}} | collective-permute-start | bytes 3145736 | tf_op jit(solution)/shard_map/ppermute | solution.py:643
  (38 other events, 1150.3 us)
